TPU v7x, 512 devices: a whole 4x8x8 slice. The times are simulated.
512 devices in a mesh: section: 2 (over z_lo), wrow: 16 (over y, core), wcol: 16 (over x, z_hi).
Axes of the slice: x: 4, y: 8, z: 8 (z_hi: 4, z_lo: 2; z = z_hi * 2 + z_lo), core: 2. Of those that a mesh axis runs over, the one named last changes fastest.
Arguments:
- states: bfloat16 [2, 256, 256, 1536], P(None, 'wrow', 'wcol'), may hold values from -6 to 6
- timesteps: int32 [2], replicated, may hold values from 0 to 999, as said below
- shifts: int32 [2, 2], P('section'), may hold values from 1 to 4
- qkv_weight: bfloat16 [2, 1536, 2304], P('section', None, 'wcol'), may hold values from -0.15625 to 0.15625
- out_weight: bfloat16 [2, 768, 1536], P('section', None, 'wcol'), may hold values from -0.21875 to 0.21875
- mod_weight: bfloat16 [2, 256, 4608], P('section', None, 'wcol'), may hold values from -0.375 to 0.375
Outputs:
- layer_states: bfloat16 [2, 2, 256, 256, 1536], P('section', None, 'wrow', 'wcol')
Inputs may be any that keep to these rules, and one draw needn't show every extreme that they name: The 2 timesteps are distinct.
All inputs are finite; a program needn't handle non-finite values.
Results may differ from a plain program's by a relative error of at most 0.0053.
Values may be sent and summed in bfloat16 or wider, within the bound.
A program may use at most 128 MiB of HBM per device.

v0:
```python
import math

import jax
import jax.numpy as jnp
from jax import lax
from jax.sharding import PartitionSpec as P

HEADS = 6
HD = 128
TEMB = 256
WIN = 8
MB = 2


epsilon = 1e-06


def passed_along(shard, axis, by):
    devices = lax.axis_size(axis)
    return lax.ppermute(shard, axis, [(i, (i + by) % devices) for i in range(devices)])


def from_behind(shard, axis, by):
    devices = lax.axis_size(axis)
    pairs = [(i, i + by) for i in range(devices) if 0 <= i + by < devices]
    return lax.ppermute(shard, axis, pairs)


def sinusoid(moments, entries):
    half_count = entries // 2
    frequency = jnp.exp(-math.log(10000.0) * jnp.arange(half_count, dtype=jnp.float32) / half_count)
    angles = moments.astype(jnp.float32)[:, None] * frequency[None, :]
    return jnp.concatenate([jnp.cos(angles), jnp.sin(angles)], axis=1)


def rounded(number):
    return lax.optimization_barrier(number.astype(jnp.bfloat16)).astype(jnp.float32)


def layer_norm(region):
    values = region.astype(jnp.float32)
    center = values - jnp.mean(values, axis=-1, keepdims=True)
    spread = jnp.mean(center * center, axis=-1, keepdims=True)
    return center * lax.rsqrt(spread + epsilon)


def window_attention(triples):
    tile_rows, tile_cols, feature_width = triples.shape
    windowed = triples.reshape(tile_rows // WIN, WIN, tile_cols // WIN, WIN, 3, HEADS, HD)
    windowed = windowed.transpose(4, 0, 2, 5, 1, 3, 6).reshape(
        3, tile_rows // WIN * (tile_cols // WIN), HEADS, WIN * WIN, HD
    )
    scores = jnp.einsum(
        "nhqd,nhkd->nhqk", windowed[0], windowed[1], preferred_element_type=jnp.float32
    ) * HD ** (-0.5)
    weights = jnp.exp(scores)
    probabilities = (weights / jnp.sum(weights, axis=-1, keepdims=True)).astype(jnp.bfloat16)
    attended = jnp.einsum(
        "nhqk,nhkd->nhqd", probabilities, windowed[2], preferred_element_type=jnp.float32
    ).astype(jnp.bfloat16)
    attended = attended.reshape(tile_rows // WIN, tile_cols // WIN, HEADS, WIN, WIN, HD).transpose(
        0, 3, 1, 4, 2, 5
    )
    return attended.reshape(tile_rows, tile_cols, HEADS * HD)


def project(region, matrix):
    tile_rows, tile_cols, feature_width = region.shape
    product = jnp.dot(
        region.reshape(tile_rows * tile_cols, feature_width),
        matrix,
        preferred_element_type=jnp.float32,
    )
    return product.reshape(tile_rows, tile_cols, -1)


def splice(region, border, amount, direction, margin, axis_index):
    if direction > 0:
        longer = jnp.concatenate([region, border], axis=axis_index)
        offset = amount
    else:
        longer = jnp.concatenate([border, region], axis=axis_index)
        offset = margin - amount
    return lax.dynamic_slice_in_dim(longer, offset, region.shape[axis_index], axis_index)


def wrap_rim(region, row_shift, col_shift, direction):
    margin = WIN // 2
    if direction > 0:
        border = region[:margin]
    else:
        border = region[region.shape[0] - margin :]
    border = passed_along(border, "wrow", -direction)
    region = splice(region, border, row_shift, direction, margin, 0)
    if direction > 0:
        border = region[:, :margin]
    else:
        border = region[:, region.shape[1] - margin :]
    border = passed_along(border, "wcol", -direction)
    return splice(region, border, col_shift, direction, margin, 1)


def shifted_layer(inputs, modulation, row_shift, col_shift, qkv_matrix, out_matrix):
    feature_width = inputs.shape[-1]
    mod_shift = modulation[:feature_width]
    mod_scale = modulation[feature_width : 2 * feature_width]
    mod_gate = modulation[2 * feature_width :]
    normed = (layer_norm(inputs) * (1.0 + mod_scale) + mod_shift).astype(jnp.bfloat16)
    triples = project(normed, qkv_matrix).astype(jnp.bfloat16)
    triples = wrap_rim(triples, row_shift, col_shift, 1)
    attended = window_attention(triples)
    restored = wrap_rim(attended, row_shift, col_shift, -1)
    projection = rounded(project(restored, out_matrix))
    return (inputs.astype(jnp.float32) + mod_gate * projection).astype(jnp.bfloat16)


def per_device(states, timesteps, shifts, qkv_weight, out_weight, mod_weight):
    embedding = jax.nn.silu(sinusoid(timesteps, TEMB)).astype(jnp.bfloat16)
    mod_part = jnp.dot(embedding, mod_weight[0], preferred_element_type=jnp.float32).astype(
        jnp.bfloat16
    )
    qkv_full, out_full, modulations = (
        lax.all_gather(qkv_weight[0], "wcol", axis=1, tiled=True),
        lax.all_gather(out_weight[0], "wcol", axis=1, tiled=True),
        lax.all_gather(mod_part, "wcol", axis=1, tiled=True),
    )
    section_index = lax.axis_index("section")
    moments = MB + lax.axis_size("section") - 1
    row_shift = shifts[0, 0]
    col_shift = shifts[0, 1]
    incoming = jnp.zeros_like(states[0])
    results = jnp.zeros_like(states)
    for moment in range(moments):
        member = moment - section_index
        batch_slot = jnp.clip(member, 0, MB - 1)
        block_input = jnp.where(section_index == 0, states[min(moment, MB - 1)], incoming)
        modulation = lax.dynamic_index_in_dim(modulations, batch_slot, 0, keepdims=False).astype(
            jnp.float32
        )
        outgoing = shifted_layer(block_input, modulation, row_shift, col_shift, qkv_full, out_full)
        active = (member >= 0) & (member < MB)
        updated = lax.dynamic_update_index_in_dim(results, outgoing, batch_slot, 0)
        results = jnp.where(active, updated, results)
        if moment + 1 < moments:
            incoming = from_behind(outgoing, "section", 1)
    return results[None]


def solution(mesh):
    in_specs = (
        P(None, "wrow", "wcol", None),
        P(),
        P("section", None),
        P("section", None, "wcol"),
        P("section", None, "wcol"),
        P("section", None, "wcol"),
    )
    out_specs = P("section", None, "wrow", "wcol", None)
    return jax.shard_map(
        per_device, mesh=mesh, in_specs=in_specs, out_specs=out_specs, check_vma=False
    )
```

profile of v0, /device:TPU:80, one launch (start us, length us, event | category | flops | bytes accessed | tf_op | source)
XLA Modules:
  0.0 355.2 jit_solution(15052046992255427230)
XLA Ops:
  6.5 0.7 all-gather.6.cloned.1.call-update
  9.0 49.1 %all-gather.2 = bf16[16,288,2]{1,2,0:T(2,128)(2,1)S(1)} all-gather(bf16[1,288,2]{1,2,0:T(2,128)(2,1)S(1)} %fusion.50), channel_id=1, replica_groups=mesh['section'=2,'wrow'=16,'wcol'=16] {'wcol'}, dimensions={0}, use_global_device_ids=true | all-gather | bytes 19584 | tf_op jit(solution)/shard_map/all_gather | solution.py:125
  58.3 1.4 convert_reduce_fusion.2
  60.0 63.6 %all-gather.6.cloned.1.call-done = bf16[1,1536,2304]{1,2,0:T(8,128)(2,1)} async-done(((bf16[1,1536,144]{1,2,0:T(8,128)(2,1)}), bf16[1,1536,2304]{1,2,0:T(8,128)(2,1)}) %all-gather.6.cloned.1.call-update) | async-done | bytes 7077904 | tf_op jit(solution)/shard_map/all_gather | solution.py:123
  123.7 5.2 %fusion.6 = bf16[16,16,2304]{2,1,0:T(8,128)(2,1)S(1)} fusion(bf16[1,1536,2304]{1,2,0:T(8,128)(2,1)} %all-gather.6.cloned.1.call-done, f32[1536]{0:T(1024)S(1)} %get-tuple-element.12, f32[1536]{0:T(1024)S(1)} %get-tuple-element.13, f32[16,16]{1,0:T(8,128)S(1)} %add_rsqrt_fusion.2, f32[16,16]{1,0:T(8,128)S(1)} %broadcast_multiply_fusion.2, ...), kind=kOutput, calls=%fused_computation.6 | convolution fusion | flops 1815281664 | bytes 9076737 | tf_op jit(solution)/shard_map/dot_general | solution.py:69
  128.9 1.0 copy-done.6
  132.5 1.7 collective-permute-done
  134.2 1.5 fusion.46
  135.7 5.7 %collective-permute-start.1 = (bf16[16,4,2304]{2,1,0:T(4,128)(2,1)S(1)}, bf16[16,4,2304]{2,1,0:T(4,128)(2,1)S(1)}, u32[]{:S(2)}, u32[]{:S(2)}) collective-permute-start(bf16[16,4,2304]{2,1,0:T(4,128)(2,1)S(1)} %slice.177), channel_id=1, source_target_pairs={{0,15},{1,0},{2,1},{3,2},{4,3},{5,4},{6,5},{7,6},{8,7},{9,8},{10,9... | collective-permute-start | bytes 884744 | tf_op jit(solution)/shard_map/ppermute | solution.py:20
  143.5 6.3 %collective-permute-done.1 = bf16[16,4,2304]{2,1,0:T(4,128)(2,1)S(1)} collective-permute-done((bf16[16,4,2304]{2,1,0:T(4,128)(2,1)S(1)}, bf16[16,4,2304]{2,1,0:T(4,128)(2,1)S(1)}, u32[]{:S(2)}, u32[]{:S(2)}) %collective-permute-start.1) | collective-permute-done | bytes 294944 | tf_op jit(solution)/shard_map/ppermute | solution.py:20
  149.8 0.9 fusion.49
  151.8 9.2 %collective-permute-start.2 = (bf16[4,16,768]{2,1,0:T(8,128)(2,1)S(1)}, bf16[4,16,768]{2,1,0:T(8,128)(2,1)S(1)}, u32[]{:S(2)}, u32[]{:S(2)}) collective-permute-start(bf16[4,16,768]{2,1,0:T(8,128)(2,1)S(1)} %slice.181), channel_id=1, source_target_pairs={{0,16},{16,32},{32,48},{48,64},{64,80},{80,96},{96,112},{112,128},... | collective-permute-start | bytes 294920 | tf_op jit(solution)/shard_map/ppermute | solution.py:20
  162.3 1.2 collective-permute-done.2
  163.6 5.1 %collective-permute-start.3 = (bf16[16,4,768]{2,1,0:T(4,128)(2,1)S(1)}, bf16[16,4,768]{2,1,0:T(4,128)(2,1)S(1)}, u32[]{:S(2)}, u32[]{:S(2)}) collective-permute-start(bf16[16,4,768]{2,1,0:T(4,128)(2,1)S(1)} %slice.182), channel_id=1, source_target_pairs={{0,1},{1,2},{2,3},{3,4},{4,5},{5,6},{6,7},{7,8},{8,9},{9,10},{10,1... | collective-permute-start | bytes 294920 | tf_op jit(solution)/shard_map/ppermute | solution.py:20
  170.1 26.3 %all-gather.8.cloned.1.call-done = bf16[1,768,1536]{1,2,0:T(8,128)(2,1)} async-done(((bf16[1,768,96]{1,2,0:T(8,128)(2,1)}), bf16[1,768,1536]{1,2,0:T(8,128)(2,1)}) %all-gather.8.cloned.1.call-update) | async-done | bytes 2359312 | tf_op jit(solution)/shard_map/all_gather | solution.py:124
  196.4 2.5 convolution_convert_fusion.2
  199.5 1.3 collective-permute-start.4
  200.8 19.2 %collective-permute-done.4 = bf16[16,16,1536]{2,1,0:T(8,128)(2,1)S(1)} collective-permute-done((bf16[16,16,1536]{2,1,0:T(8,128)(2,1)S(1)}, bf16[16,16,1536]{2,1,0:T(8,128)(2,1)S(1)}, u32[]{:S(2)}, u32[]{:S(2)}) %collective-permute-start.4) | collective-permute-done | bytes 786464 | tf_op jit(solution)/shard_map/ppermute | solution.py:26
  220.7 5.2 %fusion.9 = bf16[16,16,2304]{2,1,0:T(8,128)(2,1)S(1)} fusion(bf16[1,1536,2304]{1,2,0:T(8,128)(2,1)} %all-gather.6.cloned.1.call-done, bf16[16,16,1536]{2,1,0:T(8,128)(2,1)S(1)} %get-tuple-element.19, f32[1536]{0:T(1024)S(1)} %get-tuple-element.9, f32[1536]{0:T(1024)S(1)} %get-tuple-element.10, f32[16,16]{1,0:T(8,128)S(1)} %add_rsqrt_fusion.1, ...), kind=kOutput, calls=%fused_computation.7 | convolution fusion | flops 1814888448 | bytes 9058304 | tf_op jit(solution)/shard_map/dot_general | solution.py:69
  225.9 4.2 %collective-permute-done.5 = bf16[4,16,2304]{2,1,0:T(8,128)(2,1)S(1)} collective-permute-done((bf16[4,16,2304]{2,1,0:T(8,128)(2,1)S(1)}, bf16[4,16,2304]{2,1,0:T(8,128)(2,1)S(1)}, u32[]{:S(2)}, u32[]{:S(2)}) %collective-permute-start.5) | collective-permute-done | bytes 294944 | tf_op jit(solution)/shard_map/ppermute | solution.py:20
  230.6 5.8 %collective-permute-start.6 = (bf16[16,4,2304]{2,1,0:T(4,128)(2,1)S(1)}, bf16[16,4,2304]{2,1,0:T(4,128)(2,1)S(1)}, u32[]{:S(2)}, u32[]{:S(2)}) collective-permute-start(bf16[16,4,2304]{2,1,0:T(4,128)(2,1)S(1)} %slice.187), channel_id=1, source_target_pairs={{0,15},{1,0},{2,1},{3,2},{4,3},{5,4},{6,5},{7,6},{8,7},{9,8},{10,9... | collective-permute-start | bytes 884744 | tf_op jit(solution)/shard_map/ppermute | solution.py:20
  236.4 12.0 %collective-permute-done.6 = bf16[16,4,2304]{2,1,0:T(4,128)(2,1)S(1)} collective-permute-done((bf16[16,4,2304]{2,1,0:T(4,128)(2,1)S(1)}, bf16[16,4,2304]{2,1,0:T(4,128)(2,1)S(1)}, u32[]{:S(2)}, u32[]{:S(2)}) %collective-permute-start.6) | collective-permute-done | bytes 294944 | tf_op jit(solution)/shard_map/ppermute | solution.py:20
  248.4 0.9 fusion.48
  249.6 0.8 copy.43
  250.4 1.2 fusion.42
  251.7 2.6 convolution_convert_fusion.4
  254.3 1.1 copy.45
  255.3 1.1 collective-permute-start.7
  256.4 3.0 collective-permute-done.7
  259.5 0.7 copy-done.8
  260.3 3.5 collective-permute-start.8
  263.8 8.4 %collective-permute-done.8 = bf16[16,4,768]{2,1,0:T(4,128)(2,1)} collective-permute-done((bf16[16,4,768]{2,1,0:T(4,128)(2,1)S(1)}, bf16[16,4,768]{2,1,0:T(4,128)(2,1)}, u32[]{:S(2)}, u32[]{:S(2)}) %collective-permute-start.8) | collective-permute-done | bytes 98336 | tf_op jit(solution)/shard_map/ppermute | solution.py:20
  272.1 2.7 convolution_convert_fusion.1
  275.3 1.3 collective-permute-start.9
  276.7 19.8 %collective-permute-done.9 = bf16[16,16,1536]{2,1,0:T(8,128)(2,1)S(1)} collective-permute-done((bf16[16,16,1536]{2,1,0:T(8,128)(2,1)S(1)}, bf16[16,16,1536]{2,1,0:T(8,128)(2,1)S(1)}, u32[]{:S(2)}, u32[]{:S(2)}) %collective-permute-start.9) | collective-permute-done | bytes 786464 | tf_op jit(solution)/shard_map/ppermute | solution.py:26
  297.2 5.2 %fusion.12 = bf16[16,16,2304]{2,1,0:T(8,128)(2,1)S(1)} fusion(bf16[1,1536,2304]{1,2,0:T(8,128)(2,1)} %all-gather.6.cloned.1.call-done, bf16[16,16,1536]{2,1,0:T(8,128)(2,1)S(1)} %get-tuple-element.15, f32[1536]{0:T(1024)S(1)} %get-tuple-element.6, f32[1536]{0:T(1024)S(1)} %get-tuple-element.7, f32[16,16]{1,0:T(8,128)S(1)} %add_rsqrt_fusion, ...), kind=kOutput, calls=%fused_computation.8 | convolution fusion | flops 1814888448 | bytes 9058304 | tf_op jit(solution)/shard_map/dot_general | solution.py:69
  302.4 4.2 %collective-permute-done.10 = bf16[4,16,2304]{2,1,0:T(8,128)(2,1)S(1)} collective-permute-done((bf16[4,16,2304]{2,1,0:T(8,128)(2,1)S(1)}, bf16[4,16,2304]{2,1,0:T(8,128)(2,1)S(1)}, u32[]{:S(2)}, u32[]{:S(2)}) %collective-permute-start.10) | collective-permute-done | bytes 294944 | tf_op jit(solution)/shard_map/ppermute | solution.py:20
  307.0 3.9 %collective-permute-start.11 = (bf16[16,4,2304]{2,1,0:T(4,128)(2,1)S(1)}, bf16[16,4,2304]{2,1,0:T(4,128)(2,1)S(1)}, u32[]{:S(2)}, u32[]{:S(2)}) collective-permute-start(bf16[16,4,2304]{2,1,0:T(4,128)(2,1)S(1)} %slice.197), channel_id=1, source_target_pairs={{0,15},{1,0},{2,1},{3,2},{4,3},{5,4},{6,5},{7,6},{8,7},{9,8},{10,9... | collective-permute-start | bytes 884744 | tf_op jit(solution)/shard_map/ppermute | solution.py:20
  310.9 13.1 %collective-permute-done.11 = bf16[16,4,2304]{2,1,0:T(4,128)(2,1)S(1)} collective-permute-done((bf16[16,4,2304]{2,1,0:T(4,128)(2,1)S(1)}, bf16[16,4,2304]{2,1,0:T(4,128)(2,1)S(1)}, u32[]{:S(2)}, u32[]{:S(2)}) %collective-permute-start.11) | collective-permute-done | bytes 294944 | tf_op jit(solution)/shard_map/ppermute | solution.py:20
  324.0 0.9 fusion.47
  325.3 1.2 fusion.41
  326.5 1.7 convolution_convert_fusion.3
  328.4 4.0 %collective-permute-done.12 = bf16[4,16,768]{2,1,0:T(8,128)(2,1)S(1)} collective-permute-done((bf16[4,16,768]{2,1,0:T(8,128)(2,1)S(1)}, bf16[4,16,768]{2,1,0:T(8,128)(2,1)S(1)}, u32[]{:S(2)}, u32[]{:S(2)}) %collective-permute-start.12) | collective-permute-done | bytes 98336 | tf_op jit(solution)/shard_map/ppermute | solution.py:20
  332.5 1.9 collective-permute-start.13
  334.5 1.1 copy.56
  335.6 9.6 %collective-permute-done.13 = bf16[16,4,768]{2,1,0:T(4,128)(2,1)S(1)} collective-permute-done((bf16[16,4,768]{2,1,0:T(4,128)(2,1)S(1)}, bf16[16,4,768]{2,1,0:T(4,128)(2,1)S(1)}, u32[]{:S(2)}, u32[]{:S(2)}) %collective-permute-start.13) | collective-permute-done | bytes 98336 | tf_op jit(solution)/shard_map/ppermute | solution.py:20
  345.3 1.8 convolution_convert_fusion
  347.1 1.3 fusion.54
  (85 shorter events, 8.6 us)
Async XLA Ops:
  6.5 2.3 copy-start
  6.5 53.1 %copy-start.1 = (bf16[2,16,16,1536]{3,2,1,0:T(8,128)(2,1)S(1)}, bf16[2,16,16,1536]{3,2,1,0:T(8,128)(2,1)}, u32[]{:S(2)}) copy-start(bf16[2,16,16,1536]{3,2,1,0:T(8,128)(2,1)} %param.6) | copy-start | bytes 4718596
  6.5 117.1 %all-gather.6.cloned.1.call-start = ((), (), s32[]{:S(2)}) async-start(), calls=%async_computation | async-start | bytes 7520256 | tf_op jit(solution)/shard_map/all_gather | solution.py:123
  7.3 189.1 %all-gather.8.cloned.1.call-start = ((), (), s32[]{:S(2)}) async-start(), calls=%async_computation.1 | async-start | bytes 2506752 | tf_op jit(solution)/shard_map/all_gather | solution.py:124
  123.7 6.3 %copy-start.9 = (s32[1,2]{1,0:T(1,128)S(1)}, s32[1,2]{1,0:T(1,128)}, u32[]{:S(2)}) copy-start(s32[1,2]{1,0:T(1,128)} %param.8) | copy-start | bytes 28
  128.9 1.0 copy-start.6
  129.9 4.3 %collective-permute-start = (bf16[4,16,2304]{2,1,0:T(8,128)(2,1)S(1)}, bf16[4,16,2304]{2,1,0:T(8,128)(2,1)S(1)}, u32[]{:S(2)}, u32[]{:S(2)}) collective-permute-start(bf16[4,16,2304]{2,1,0:T(8,128)(2,1)S(1)} %slice.176), channel_id=1, source_target_pairs={{0,240},{16,0},{32,16},{48,32},{64,48},{80,64},{96,80},{112,96},{1... | collective-permute-start | bytes 884744 | tf_op jit(solution)/shard_map/ppermute | solution.py:20
  135.7 14.0 %collective-permute-start.1 = (bf16[16,4,2304]{2,1,0:T(4,128)(2,1)S(1)}, bf16[16,4,2304]{2,1,0:T(4,128)(2,1)S(1)}, u32[]{:S(2)}, u32[]{:S(2)}) collective-permute-start(bf16[16,4,2304]{2,1,0:T(4,128)(2,1)S(1)} %slice.177), channel_id=1, source_target_pairs={{0,15},{1,0},{2,1},{3,2},{4,3},{5,4},{6,5},{7,6},{8,7},{9,8},{10,9... | collective-permute-start | bytes 884744 | tf_op jit(solution)/shard_map/ppermute | solution.py:20
  151.8 11.6 %collective-permute-start.2 = (bf16[4,16,768]{2,1,0:T(8,128)(2,1)S(1)}, bf16[4,16,768]{2,1,0:T(8,128)(2,1)S(1)}, u32[]{:S(2)}, u32[]{:S(2)}) collective-permute-start(bf16[4,16,768]{2,1,0:T(8,128)(2,1)S(1)} %slice.181), channel_id=1, source_target_pairs={{0,16},{16,32},{32,48},{48,64},{64,80},{80,96},{96,112},{112,128},... | collective-permute-start | bytes 294920 | tf_op jit(solution)/shard_map/ppermute | solution.py:20
  163.6 32.8 %collective-permute-start.3 = (bf16[16,4,768]{2,1,0:T(4,128)(2,1)S(1)}, bf16[16,4,768]{2,1,0:T(4,128)(2,1)S(1)}, u32[]{:S(2)}, u32[]{:S(2)}) collective-permute-start(bf16[16,4,768]{2,1,0:T(4,128)(2,1)S(1)} %slice.182), channel_id=1, source_target_pairs={{0,1},{1,2},{2,3},{3,4},{4,5},{5,6},{6,7},{7,8},{8,9},{9,10},{10,1... | collective-permute-start | bytes 294920 | tf_op jit(solution)/shard_map/ppermute | solution.py:20
  199.5 20.6 %collective-permute-start.4 = (bf16[16,16,1536]{2,1,0:T(8,128)(2,1)S(1)}, bf16[16,16,1536]{2,1,0:T(8,128)(2,1)S(1)}, u32[]{:S(2)}, u32[]{:S(2)}) collective-permute-start(bf16[16,16,1536]{2,1,0:T(8,128)(2,1)S(1)} %get-tuple-element.21), channel_id=1, source_target_pairs={{0,256},{1,257},{2,258},{3,259},{4,260},{5,261},{6,262},{7,263},{8... | collective-permute-start | bytes 2359304 | tf_op jit(solution)/shard_map/ppermute | solution.py:26
  220.3 5.6 %copy-start.4 = (bf16[16,16,1536]{2,1,0:T(8,128)(2,1)}, bf16[16,16,1536]{2,1,0:T(8,128)(2,1)S(1)}, u32[]{:S(2)}) copy-start(bf16[16,16,1536]{2,1,0:T(8,128)(2,1)S(1)} %get-tuple-element.19) | copy-start | bytes 2359300
  225.9 4.3 %collective-permute-start.5 = (bf16[4,16,2304]{2,1,0:T(8,128)(2,1)S(1)}, bf16[4,16,2304]{2,1,0:T(8,128)(2,1)S(1)}, u32[]{:S(2)}, u32[]{:S(2)}) collective-permute-start(bf16[4,16,2304]{2,1,0:T(8,128)(2,1)S(1)} %slice.186), channel_id=1, source_target_pairs={{0,240},{16,0},{32,16},{48,32},{64,48},{80,64},{96,80},{112,96},{1... | collective-permute-start | bytes 884744 | tf_op jit(solution)/shard_map/ppermute | solution.py:20
  230.6 17.8 %collective-permute-start.6 = (bf16[16,4,2304]{2,1,0:T(4,128)(2,1)S(1)}, bf16[16,4,2304]{2,1,0:T(4,128)(2,1)S(1)}, u32[]{:S(2)}, u32[]{:S(2)}) collective-permute-start(bf16[16,4,2304]{2,1,0:T(4,128)(2,1)S(1)} %slice.187), channel_id=1, source_target_pairs={{0,15},{1,0},{2,1},{3,2},{4,3},{5,4},{6,5},{7,6},{8,7},{9,8},{10,9... | collective-permute-start | bytes 884744 | tf_op jit(solution)/shard_map/ppermute | solution.py:20
  255.3 4.1 %collective-permute-start.7 = (bf16[4,16,768]{2,1,0:T(8,128)(2,1)S(1)}, bf16[4,16,768]{2,1,0:T(8,128)(2,1)S(1)}, u32[]{:S(2)}, u32[]{:S(2)}) collective-permute-start(bf16[4,16,768]{2,1,0:T(8,128)(2,1)S(1)} %slice.191), channel_id=1, source_target_pairs={{0,16},{16,32},{32,48},{48,64},{64,80},{80,96},{96,112},{112,128},... | collective-permute-start | bytes 294920 | tf_op jit(solution)/shard_map/ppermute | solution.py:20
  259.5 0.7 copy-start.8
  260.3 11.9 %collective-permute-start.8 = (bf16[16,4,768]{2,1,0:T(4,128)(2,1)S(1)}, bf16[16,4,768]{2,1,0:T(4,128)(2,1)}, u32[]{:S(2)}, u32[]{:S(2)}) collective-permute-start(bf16[16,4,768]{2,1,0:T(4,128)(2,1)S(1)} %slice.192), channel_id=1, source_target_pairs={{0,1},{1,2},{2,3},{3,4},{4,5},{5,6},{6,7},{7,8},{8,9},{9,10},{10,1... | collective-permute-start | bytes 294920 | tf_op jit(solution)/shard_map/ppermute | solution.py:20
  263.8 11.0 %copy-start.5 = (bf16[16,16,1536]{2,1,0:T(8,128)(2,1)S(1)}, bf16[16,16,1536]{2,1,0:T(8,128)(2,1)}, u32[]{:S(2)}) copy-start(bf16[16,16,1536]{2,1,0:T(8,128)(2,1)} %copy-done.4) | copy-start | bytes 2359300
  275.3 21.2 %collective-permute-start.9 = (bf16[16,16,1536]{2,1,0:T(8,128)(2,1)S(1)}, bf16[16,16,1536]{2,1,0:T(8,128)(2,1)S(1)}, u32[]{:S(2)}, u32[]{:S(2)}) collective-permute-start(bf16[16,16,1536]{2,1,0:T(8,128)(2,1)S(1)} %get-tuple-element.17), channel_id=1, source_target_pairs={{0,256},{1,257},{2,258},{3,259},{4,260},{5,261},{6,262},{7,263},{8... | collective-permute-start | bytes 2359304 | tf_op jit(solution)/shard_map/ppermute | solution.py:26
  296.8 5.6 %copy-start.2 = (bf16[16,16,1536]{2,1,0:T(8,128)(2,1)}, bf16[16,16,1536]{2,1,0:T(8,128)(2,1)S(1)}, u32[]{:S(2)}) copy-start(bf16[16,16,1536]{2,1,0:T(8,128)(2,1)S(1)} %get-tuple-element.15) | copy-start | bytes 2359300
  302.4 4.3 %collective-permute-start.10 = (bf16[4,16,2304]{2,1,0:T(8,128)(2,1)S(1)}, bf16[4,16,2304]{2,1,0:T(8,128)(2,1)S(1)}, u32[]{:S(2)}, u32[]{:S(2)}) collective-permute-start(bf16[4,16,2304]{2,1,0:T(8,128)(2,1)S(1)} %slice.196), channel_id=1, source_target_pairs={{0,240},{16,0},{32,16},{48,32},{64,48},{80,64},{96,80},{112,96},{1... | collective-permute-start | bytes 884744 | tf_op jit(solution)/shard_map/ppermute | solution.py:20
  307.0 17.0 %collective-permute-start.11 = (bf16[16,4,2304]{2,1,0:T(4,128)(2,1)S(1)}, bf16[16,4,2304]{2,1,0:T(4,128)(2,1)S(1)}, u32[]{:S(2)}, u32[]{:S(2)}) collective-permute-start(bf16[16,4,2304]{2,1,0:T(4,128)(2,1)S(1)} %slice.197), channel_id=1, source_target_pairs={{0,15},{1,0},{2,1},{3,2},{4,3},{5,4},{6,5},{7,6},{8,7},{9,8},{10,9... | collective-permute-start | bytes 884744 | tf_op jit(solution)/shard_map/ppermute | solution.py:20
  328.3 4.1 %collective-permute-start.12 = (bf16[4,16,768]{2,1,0:T(8,128)(2,1)S(1)}, bf16[4,16,768]{2,1,0:T(8,128)(2,1)S(1)}, u32[]{:S(2)}, u32[]{:S(2)}) collective-permute-start(bf16[4,16,768]{2,1,0:T(8,128)(2,1)S(1)} %slice.201), channel_id=1, source_target_pairs={{0,16},{16,32},{32,48},{48,64},{64,80},{80,96},{96,112},{112,128},... | collective-permute-start | bytes 294920 | tf_op jit(solution)/shard_map/ppermute | solution.py:20
  332.5 2.0 copy-start.7
  332.5 12.7 %collective-permute-start.13 = (bf16[16,4,768]{2,1,0:T(4,128)(2,1)S(1)}, bf16[16,4,768]{2,1,0:T(4,128)(2,1)S(1)}, u32[]{:S(2)}, u32[]{:S(2)}) collective-permute-start(bf16[16,4,768]{2,1,0:T(4,128)(2,1)S(1)} %slice.202), channel_id=1, source_target_pairs={{0,1},{1,2},{2,3},{3,4},{4,5},{5,6},{6,7},{7,8},{8,9},{9,10},{10,1... | collective-permute-start | bytes 294920 | tf_op jit(solution)/shard_map/ppermute | solution.py:20
  334.5 10.8 %copy-start.10 = (bf16[1,768,1536]{1,2,0:T(8,128)(2,1)S(1)}, bf16[1,768,1536]{1,2,0:T(8,128)(2,1)}, u32[]{:S(2)}) copy-start(bf16[1,768,1536]{1,2,0:T(8,128)(2,1)} %all-gather.8.cloned.1.call-done) | copy-start | bytes 7077892
  335.6 11.5 %copy-start.3 = (bf16[16,16,1536]{2,1,0:T(8,128)(2,1)S(1)}, bf16[16,16,1536]{2,1,0:T(8,128)(2,1)}, u32[]{:S(2)}) copy-start(bf16[16,16,1536]{2,1,0:T(8,128)(2,1)} %copy-done.2) | copy-start | bytes 2359300
Sparse Core Ops, SparseCore 0:
  10.4 113.2 all-gather.5
  126.7 69.5 all-gather.7
where the time goes:
time: 357 us; the launch traced here: 355 us
  waiting for transfers between devices  198 us (55%)
  blocking collectives  49.1 us (14%)
  starting transfers between devices  38.9 us (11%)
  matrix products  30.1 us (8%)
  between operations  20.5 us (6%)
  other arithmetic  11 us (3%)
  local copies, waits for them, and re-layouts  7.45 us (2%)
    ppermute x12, waiting for transfers between devices, passed_along(): lax.ppermute(shard, axis, [(i, (i + by) % devices) for i in range(devices)])  67.7 us
    all_gather x1, waiting for transfers between devices, per_device(): lax.all_gather(qkv_weight[0], 'wcol', axis=1, tiled=True)  63.6 us
    all_gather x1, blocking collectives, per_device(): lax.all_gather(mod_part, 'wcol', axis=1, tiled=True)  49.1 us
    ppermute x2, waiting for transfers between devices, from_behind(): return lax.ppermute(shard, axis, pairs)  39 us
    ppermute x12, starting transfers between devices, passed_along(): lax.ppermute(shard, axis, [(i, (i + by) % devices) for i in range(devices)])  36.3 us
    all_gather x1, waiting for transfers between devices, per_device(): lax.all_gather(out_weight[0], 'wcol', axis=1, tiled=True)  26.3 us
    dot_general x6, matrix products, project(): jnp.dot(region.reshape(tile_rows * tile_cols, feature_width), matrix, pre...  22.5 us
  transfers between devices with their start and end apart: 16, of which 15 were waited for; matrix products, arithmetic and copies ran while one was open for 4% of the time, Pallas kernels for 0%

commit v1 on v0

--- a/solution.py
+++ b/solution.py
@@ -1,8 +1,11 @@
+import functools
 import math
 
 import jax
 import jax.numpy as jnp
 from jax import lax
+from jax.experimental import pallas as pl
+from jax.experimental.pallas import tpu as pltpu
 from jax.sharding import PartitionSpec as P
 
 HEADS = 6
@@ -10,6 +13,8 @@
 TEMB = 256
 WIN = 8
 MB = 2
+MESH = pl.DeviceIdType.MESH
+UNIT = 48
 
 
 epsilon = 1e-06
@@ -64,11 +69,12 @@
     return attended.reshape(tile_rows, tile_cols, HEADS * HD)
 
 
-def project(region, matrix):
+def project(region, matrix_t):
     tile_rows, tile_cols, feature_width = region.shape
-    product = jnp.dot(
+    product = lax.dot_general(
         region.reshape(tile_rows * tile_cols, feature_width),
-        matrix,
+        matrix_t,
+        (((1,), (1,)), ((), ())),
         preferred_element_type=jnp.float32,
     )
     return product.reshape(tile_rows, tile_cols, -1)
@@ -100,18 +106,215 @@
     return splice(region, border, col_shift, direction, margin, 1)
 
 
-def shifted_layer(inputs, modulation, row_shift, col_shift, qkv_matrix, out_matrix):
+def shifted_layer(inputs, modulation, row_shift, col_shift, qkv_t, out_t):
     feature_width = inputs.shape[-1]
     mod_shift = modulation[:feature_width]
     mod_scale = modulation[feature_width : 2 * feature_width]
     mod_gate = modulation[2 * feature_width :]
     normed = (layer_norm(inputs) * (1.0 + mod_scale) + mod_shift).astype(jnp.bfloat16)
-    triples = project(normed, qkv_matrix).astype(jnp.bfloat16)
+    triples = project(normed, qkv_t).astype(jnp.bfloat16)
     triples = wrap_rim(triples, row_shift, col_shift, 1)
     attended = window_attention(triples)
     restored = wrap_rim(attended, row_shift, col_shift, -1)
-    projection = rounded(project(restored, out_matrix))
+    projection = rounded(project(restored, out_t))
     return (inputs.astype(jnp.float32) + mod_gate * projection).astype(jnp.bfloat16)
+
+
+def unit_row(w, q):
+    last = q // 3
+    return (144 * w + UNIT * q) * (1 - last) + (2304 + UNIT * w) * last
+
+
+ORDER = (
+    (0, -1), (0, 1), (-1, 0), (1, 0), (0, 2), (-1, -1), (1, -1), (-1, 1), (1, 1),
+    (-1, 2), (1, 2), (2, 0), (2, -1), (2, 1), (2, 2),
+)
+
+
+def place():
+    row, col = lax.axis_index("wrow"), lax.axis_index("wcol")
+    return row, col, row // 2, row % 2, col // 4, col % 4
+
+
+def gather_weights(comb, weights, sem_own, sem_send, sem_recv, sem_half):
+    row, col, y, core, x, z = place()
+    q = (y % 2) * 2 + core
+    counter = [0]
+    sends = []
+
+    def unit(w, quarter, first=0, count=UNIT):
+        start = pl.multiple_of(unit_row(w, quarter) + first, 16)
+        return weights.at[pl.ds(start, count), :]
+
+    def copy(w, quarter, target, slot, first=0, count=UNIT, recv=None):
+        part = unit(w, quarter, first, count)
+        return pltpu.make_async_remote_copy(
+            src_ref=part,
+            dst_ref=part,
+            send_sem=sem_send.at[slot],
+            recv_sem=sem_recv.at[w * 4 + quarter] if recv is None else recv,
+            device_id=target,
+            device_id_type=MESH,
+        )
+
+    def send(w, quarter, target, **kw):
+        c = copy(w, quarter, target, counter[0], **kw)
+        counter[0] += 1
+        c.start()
+        sends.append(c)
+
+    def arrived(w, quarter, **kw):
+        copy(w, quarter, {"wrow": row}, 0, **kw).wait_recv()
+
+    def at_col(dx, dz):
+        return {"wcol": ((x + dx + 4) % 4) * 4 + (z + dz + 4) % 4}
+
+    partner = {"wrow": y * 2 + 1 - core}
+
+    def number(dx, dz):
+        return ((x + dx + 4) % 4) * 4 + (z + dz + 4) % 4
+
+    def to_row(w):
+        up = (w // 4 + w % 4) % 2
+        return {"wrow": ((y + 7 + 2 * up) % 8) * 2 + core}
+
+    own = []
+    for quarter in range(4):
+        c = pltpu.make_async_copy(
+            comb.at[pl.ds(UNIT * quarter, UNIT), :], unit(col, quarter), sem_own.at[quarter]
+        )
+        c.start()
+        own.append(c)
+
+    def begin():
+        for c in own:
+            c.wait()
+        for d in ((0, 1), (0, -1), (1, 0), (-1, 0)):
+            send(col, q, at_col(*d))
+
+    def plane():
+        for dx, dz in ORDER:
+            w = number(dx, dz)
+            if (dx, dz) == (0, 2):
+                arrived(w, q, first=0, count=32, recv=sem_half.at[0])
+                arrived(w, q, first=32, count=16, recv=sem_half.at[1])
+            else:
+                arrived(w, q)
+            if dx == 0:
+                send(w, q, at_col(1, 0))
+                send(w, q, at_col(-1, 0))
+                if dz == -1:
+                    send(w, q, at_col(0, 1), first=0, count=32, recv=sem_half.at[0])
+                if dz == 1:
+                    send(w, q, at_col(0, -1), first=32, count=16, recv=sem_half.at[1])
+            if dx == -1 and dz in (0, -1):
+                send(w, q, at_col(1, 0))
+            if dx == 1 and dz in (1, 2):
+                send(w, q, at_col(-1, 0))
+            send(w, q, to_row(w))
+            send(w, q, partner)
+
+    def rows():
+        qy = ((y + 1) % 2) * 2 + core
+        for d in ORDER:
+            arrived(number(*d), qy)
+            send(number(*d), qy, partner)
+
+    def sides():
+        for d in ORDER:
+            arrived(number(*d), (y % 2) * 2 + 1 - core)
+        for d in ORDER:
+            arrived(number(*d), ((y + 1) % 2) * 2 + 1 - core)
+
+    def finish():
+        for c in sends:
+            c.wait_send()
+
+    return begin, plane, rows, sides, finish
+
+
+def gather_kernel(
+    comb, mod_own, w_out, mods, weights, sem_own, sem_send, sem_recv, sem_half, sem_ms, sem_mr, sem_o
+):
+    row, col, y, core, x, z = place()
+    begin, plane, rows, sides, finish = gather_weights(
+        comb, weights, sem_own, sem_send, sem_recv, sem_half
+    )
+    barrier = pltpu.get_barrier_semaphore()
+    peers = [{"wcol": (col + k) % 16} for k in range(1, 16)]
+    near = [
+        {"wrow": y * 2 + 1 - core},
+        {"wrow": ((y + 1) % 8) * 2 + core},
+        {"wrow": ((y + 7) % 8) * 2 + core},
+    ]
+    for peer in peers + near:
+        pl.semaphore_signal(barrier, inc=1, device_id=peer, device_id_type=MESH)
+    pl.semaphore_wait(barrier, 18)
+    begin()
+    mods[pl.ds(col, 1)] = mod_own[...][None]
+    msends = []
+    for k in range(1, 16):
+        c = pltpu.make_async_remote_copy(
+            src_ref=mod_own,
+            dst_ref=mods.at[col],
+            send_sem=sem_ms.at[k],
+            recv_sem=sem_mr.at[col],
+            device_id=peers[k - 1],
+            device_id_type=MESH,
+        )
+        c.start()
+        msends.append(c)
+    plane()
+    rows()
+    sides()
+    for k in range(1, 16):
+        other = (col + k) % 16
+        pltpu.make_async_remote_copy(
+            src_ref=mod_own,
+            dst_ref=mods.at[other],
+            send_sem=sem_ms.at[k],
+            recv_sem=sem_mr.at[other],
+            device_id=peers[k - 1],
+            device_id_type=MESH,
+        ).wait_recv()
+    out = pltpu.make_async_copy(weights, w_out, sem_o)
+    out.start()
+    finish()
+    for c in msends:
+        c.wait_send()
+    out.wait()
+
+
+def gather(comb, mod_own):
+    dma = pltpu.SemaphoreType.DMA
+    return pl.pallas_call(
+        gather_kernel,
+        out_shape=(
+            jax.ShapeDtypeStruct((3072, 1536), jnp.bfloat16),
+            jax.ShapeDtypeStruct((16, 24, 128), jnp.float32),
+        ),
+        in_specs=[pl.BlockSpec(memory_space=pl.ANY), pl.BlockSpec(memory_space=pltpu.VMEM)],
+        out_specs=(pl.BlockSpec(memory_space=pl.ANY), pl.BlockSpec(memory_space=pltpu.VMEM)),
+        scratch_shapes=[
+            pltpu.VMEM((3072, 1536), jnp.bfloat16),
+            dma((4,)),
+            dma((68,)),
+            dma((64,)),
+            dma((2,)),
+            dma((16,)),
+            dma((16,)),
+            dma,
+        ],
+        compiler_params=pltpu.CompilerParams(
+            collective_id=0, has_side_effects=True, vmem_limit_bytes=48 << 20
+        ),
+        name="gather",
+    )(comb, mod_own)
+
+
+def packed_modulation(mod_part):
+    pieces = mod_part.astype(jnp.float32).reshape(MB * 9, 32)
+    return jnp.pad(jnp.tile(pieces, (1, 4)), ((0, 6), (0, 0)))
 
 
 def per_device(states, timesteps, shifts, qkv_weight, out_weight, mod_weight):
@@ -119,11 +322,14 @@
     mod_part = jnp.dot(embedding, mod_weight[0], preferred_element_type=jnp.float32).astype(
         jnp.bfloat16
     )
-    qkv_full, out_full, modulations = (
-        lax.all_gather(qkv_weight[0], "wcol", axis=1, tiled=True),
-        lax.all_gather(out_weight[0], "wcol", axis=1, tiled=True),
-        lax.all_gather(mod_part, "wcol", axis=1, tiled=True),
-    )
+    out_rows = out_weight[0].T
+    comb = jnp.concatenate(
+        [qkv_weight[0].T, jnp.concatenate([out_rows[:UNIT], out_rows[UNIT:]], axis=1)], axis=0
+    )
+    weights, mods = gather(comb, packed_modulation(mod_part))
+    qkv_full = weights[:2304]
+    out_full = weights[2304:].reshape(16, UNIT, 2, 768).transpose(0, 2, 1, 3).reshape(1536, 768)
+    modulations = mods[:, :18, :32].reshape(16, MB, 9 * 32).transpose(1, 0, 2).reshape(MB, -1)
     section_index = lax.axis_index("section")
     moments = MB + lax.axis_size("section") - 1
     row_shift = shifts[0, 0]
@@ -134,9 +340,7 @@
         member = moment - section_index
         batch_slot = jnp.clip(member, 0, MB - 1)
         block_input = jnp.where(section_index == 0, states[min(moment, MB - 1)], incoming)
-        modulation = lax.dynamic_index_in_dim(modulations, batch_slot, 0, keepdims=False).astype(
-            jnp.float32
-        )
+        modulation = lax.dynamic_index_in_dim(modulations, batch_slot, 0, keepdims=False)
         outgoing = shifted_layer(block_input, modulation, row_shift, col_shift, qkv_full, out_full)
         active = (member >= 0) & (member < MB)
         updated = lax.dynamic_update_index_in_dim(results, outgoing, batch_slot, 0)

time: 357 us -> 268 us (0.75)
  the two profiles are of different devices: /device:TPU:80 before, /device:TPU:56 now
where the time goes in v1:
time: 268 us; the launch traced here: 267 us
  waiting for transfers between devices  100 us (37%)
  Pallas kernels  51.5 us (19%)
  starting transfers between devices  45.8 us (17%)
  matrix products  30.1 us (11%)
  local copies, waits for them, and re-layouts  20.5 us (8%)
  other arithmetic  12.3 us (5%)
  between operations  7.19 us (3%)
    ppermute x12, waiting for transfers between devices, passed_along(): lax.ppermute(shard, axis, [(i, (i + by) % devices) for i in range(devices)])  70.4 us
    pallas_call x1, Pallas kernels, gather(): pl.pallas_call(gather_kernel, out_shape=(jax.ShapeDtypeStruct((3072, 1536...  51.5 us
    ppermute x12, starting transfers between devices, passed_along(): lax.ppermute(shard, axis, [(i, (i + by) % devices) for i in range(devices)])  32 us
    ppermute x2, waiting for transfers between devices, from_behind(): return lax.ppermute(shard, axis, pairs)  29.6 us
    dot_general x6, matrix products, project(): lax.dot_general(region.reshape(tile_rows * tile_cols, feature_width), mat...  22.5 us
    ppermute x2, starting transfers between devices, from_behind(): return lax.ppermute(shard, axis, pairs)  13.8 us
    reshape x1, local copies, waits for them, and re-layouts, per_device(): weights[2304:].reshape(16, UNIT, 2, 768).transpose(0, 2, 1, 3)  5.97 us
  transfers between devices with their start and end apart: 14, of which 13 were waited for; matrix products, arithmetic and copies ran while one was open for 5% of the time, Pallas kernels for 0%

profile of v1, /device:TPU:56, one launch (start us, length us, event | category | flops | bytes accessed | tf_op | source)
XLA Modules:
  0.0 267.4 jit_solution(5007622295653686946)
XLA Ops:
  0.8 1.4 convert_reduce_fusion.2
  2.1 1.5 fusion.34
  4.2 51.5 %gather.1 = (bf16[3072,1536]{1,0:T(8,128)(2,1)}, f32[16,24,128]{2,1,0:T(8,128)S(1)}) custom-call(bf16[192,1536]{1,0:T(8,128)(2,1)S(1)} %maximum_maximum_fusion.comb, f32[24,128]{1,0:T(8,128)S(1)} %pad.4.mod_own), custom_call_target="tpu_custom_call" | custom-call | tf_op jit(solution)/shard_map/gather/pallas_call | solution.py:290
  56.2 5.2 %fusion.9 = bf16[16,16,2304]{2,1,0:T(8,128)(2,1)S(1)} fusion(bf16[3072,1536]{1,0:T(8,128)(2,1)} %get-tuple-element.8, f32[1536]{0:T(1024)S(1)} %get-tuple-element.17, f32[1536]{0:T(1024)S(1)} %get-tuple-element.13, f32[16,16]{1,0:T(8,128)S(1)} %add_rsqrt_fusion.2, f32[16,16]{1,0:T(8,128)S(1)} %broadcast_multiply_fusion.2, ...), kind=kOutput, calls=%fused_computation.9 | convolution fusion | flops 1815281664 | bytes 9076737 | tf_op jit(solution)/shard_map/dot_general | solution.py:74
  61.4 1.0 copy-done.7
  62.4 5.7 %collective-permute-start = (bf16[4,16,2304]{2,1,0:T(8,128)(2,1)S(1)}, bf16[4,16,2304]{2,1,0:T(8,128)(2,1)S(1)}, u32[]{:S(2)}, u32[]{:S(2)}) collective-permute-start(bf16[4,16,2304]{2,1,0:T(8,128)(2,1)S(1)} %slice.177), channel_id=1, source_target_pairs={{0,240},{16,0},{32,16},{48,32},{64,48},{80,64},{96,80},{112,96},{1... | collective-permute-start | bytes 884744 | tf_op jit(solution)/shard_map/ppermute | solution.py:25
  70.7 1.7 collective-permute-done
  72.4 1.5 fusion.46
  73.9 4.9 %collective-permute-start.1 = (bf16[16,4,2304]{2,1,0:T(4,128)(2,1)S(1)}, bf16[16,4,2304]{2,1,0:T(4,128)(2,1)S(1)}, u32[]{:S(2)}, u32[]{:S(2)}) collective-permute-start(bf16[16,4,2304]{2,1,0:T(4,128)(2,1)S(1)} %slice.178), channel_id=1, source_target_pairs={{0,15},{1,0},{2,1},{3,2},{4,3},{5,4},{6,5},{7,6},{8,7},{9,8},{10,9... | collective-permute-start | bytes 884744 | tf_op jit(solution)/shard_map/ppermute | solution.py:25
  80.8 5.5 %collective-permute-done.1 = bf16[16,4,2304]{2,1,0:T(4,128)(2,1)S(1)} collective-permute-done((bf16[16,4,2304]{2,1,0:T(4,128)(2,1)S(1)}, bf16[16,4,2304]{2,1,0:T(4,128)(2,1)S(1)}, u32[]{:S(2)}, u32[]{:S(2)}) %collective-permute-start.1) | collective-permute-done | bytes 294944 | tf_op jit(solution)/shard_map/ppermute | solution.py:25
  86.4 0.9 fusion.49
  89.7 2.8 %collective-permute-done.2 = bf16[4,16,768]{2,1,0:T(8,128)(2,1)S(1)} collective-permute-done((bf16[4,16,768]{2,1,0:T(8,128)(2,1)S(1)}, bf16[4,16,768]{2,1,0:T(8,128)(2,1)S(1)}, u32[]{:S(2)}, u32[]{:S(2)}) %collective-permute-start.2) | collective-permute-done | bytes 98336 | tf_op jit(solution)/shard_map/ppermute | solution.py:25
  92.6 3.8 %collective-permute-start.3 = (bf16[16,4,768]{2,1,0:T(4,128)(2,1)S(1)}, bf16[16,4,768]{2,1,0:T(4,128)(2,1)S(1)}, u32[]{:S(2)}, u32[]{:S(2)}) collective-permute-start(bf16[16,4,768]{2,1,0:T(4,128)(2,1)S(1)} %slice.183), channel_id=1, source_target_pairs={{0,1},{1,2},{2,3},{3,4},{4,5},{5,6},{6,7},{7,8},{8,9},{9,10},{10,1... | collective-permute-start | bytes 294920 | tf_op jit(solution)/shard_map/ppermute | solution.py:25
  97.8 3.2 %slice.153 = bf16[768,1536]{1,0:T(8,128)(2,1)} slice(bf16[3072,1536]{1,0:T(8,128)(2,1)} %get-tuple-element.8), slice={[2304:3072], [0:1536]} | slice | bytes 4718592 | tf_op jit(solution)/shard_map/slice | solution.py:331
  101.0 6.0 %reshape.213 = bf16[16,48,2,768]{3,2,1,0:T(2,128)(2,1)} reshape(bf16[768,1536]{1,0:T(8,128)(2,1)} %slice.153) | data formatting | bytes 4718592 | tf_op jit(solution)/shard_map/reshape | solution.py:331
  107.0 3.4 %copy.20 = bf16[16,2,48,768]{3,2,1,0:T(8,128)(2,1)} copy(bf16[16,2,48,768]{3,1,2,0:T(2,128)(2,1)} %bitcast.123) | data formatting | bytes 4718592 | tf_op jit(solution)/shard_map/transpose | solution.py:331
  110.5 2.5 convolution_convert_fusion.2
  113.5 9.9 %collective-permute-start.4 = (bf16[16,16,1536]{2,1,0:T(8,128)(2,1)S(1)}, bf16[16,16,1536]{2,1,0:T(8,128)(2,1)S(1)}, u32[]{:S(2)}, u32[]{:S(2)}) collective-permute-start(bf16[16,16,1536]{2,1,0:T(8,128)(2,1)S(1)} %get-tuple-element.25), channel_id=1, source_target_pairs={{0,256},{1,257},{2,258},{3,259},{4,260},{5,261},{6,262},{7,263},{8... | collective-permute-start | bytes 2359304 | tf_op jit(solution)/shard_map/ppermute | solution.py:31
  123.4 16.7 %collective-permute-done.4 = bf16[16,16,1536]{2,1,0:T(8,128)(2,1)S(1)} collective-permute-done((bf16[16,16,1536]{2,1,0:T(8,128)(2,1)S(1)}, bf16[16,16,1536]{2,1,0:T(8,128)(2,1)S(1)}, u32[]{:S(2)}, u32[]{:S(2)}) %collective-permute-start.4) | collective-permute-done | bytes 786464 | tf_op jit(solution)/shard_map/ppermute | solution.py:31
  140.8 5.2 %fusion.12 = bf16[16,16,2304]{2,1,0:T(8,128)(2,1)S(1)} fusion(bf16[3072,1536]{1,0:T(8,128)(2,1)} %get-tuple-element.8, bf16[16,16,1536]{2,1,0:T(8,128)(2,1)S(1)} %get-tuple-element.23, f32[1536]{0:T(1024)S(1)} %get-tuple-element.16, f32[1536]{0:T(1024)S(1)} %get-tuple-element.11, f32[16,16]{1,0:T(8,128)S(1)} %add_rsqrt_fusion.1, ...), kind=kOutput, calls=%fused_computation.10 | convolution fusion | flops 1814888448 | bytes 9058304 | tf_op jit(solution)/shard_map/dot_general | solution.py:74
  146.1 4.2 %collective-permute-done.5 = bf16[4,16,2304]{2,1,0:T(8,128)(2,1)S(1)} collective-permute-done((bf16[4,16,2304]{2,1,0:T(8,128)(2,1)S(1)}, bf16[4,16,2304]{2,1,0:T(8,128)(2,1)S(1)}, u32[]{:S(2)}, u32[]{:S(2)}) %collective-permute-start.5) | collective-permute-done | bytes 294944 | tf_op jit(solution)/shard_map/ppermute | solution.py:25
  150.7 6.7 %collective-permute-start.6 = (bf16[16,4,2304]{2,1,0:T(4,128)(2,1)S(1)}, bf16[16,4,2304]{2,1,0:T(4,128)(2,1)S(1)}, u32[]{:S(2)}, u32[]{:S(2)}) collective-permute-start(bf16[16,4,2304]{2,1,0:T(4,128)(2,1)S(1)} %slice.185), channel_id=1, source_target_pairs={{0,15},{1,0},{2,1},{3,2},{4,3},{5,4},{6,5},{7,6},{8,7},{9,8},{10,9... | collective-permute-start | bytes 884744 | tf_op jit(solution)/shard_map/ppermute | solution.py:25
  157.4 12.9 %collective-permute-done.6 = bf16[16,4,2304]{2,1,0:T(4,128)(2,1)S(1)} collective-permute-done((bf16[16,4,2304]{2,1,0:T(4,128)(2,1)S(1)}, bf16[16,4,2304]{2,1,0:T(4,128)(2,1)S(1)}, u32[]{:S(2)}, u32[]{:S(2)}) %collective-permute-start.6) | collective-permute-done | bytes 294944 | tf_op jit(solution)/shard_map/ppermute | solution.py:25
  170.3 0.9 fusion.48
  171.4 0.9 copy.23
  172.4 1.2 fusion.42
  173.6 2.6 convolution_convert_fusion.4
  176.3 1.1 copy.25
  177.4 1.0 collective-permute-start.7
  178.3 3.1 %collective-permute-done.7 = bf16[4,16,768]{2,1,0:T(8,128)(2,1)S(1)} collective-permute-done((bf16[4,16,768]{2,1,0:T(8,128)(2,1)S(1)}, bf16[4,16,768]{2,1,0:T(8,128)(2,1)S(1)}, u32[]{:S(2)}, u32[]{:S(2)}) %collective-permute-start.7) | collective-permute-done | bytes 98336 | tf_op jit(solution)/shard_map/ppermute | solution.py:25
  182.3 1.9 collective-permute-start.8
  184.2 9.4 %collective-permute-done.8 = bf16[16,4,768]{2,1,0:T(4,128)(2,1)S(1)} collective-permute-done((bf16[16,4,768]{2,1,0:T(4,128)(2,1)S(1)}, bf16[16,4,768]{2,1,0:T(4,128)(2,1)S(1)}, u32[]{:S(2)}, u32[]{:S(2)}) %collective-permute-start.8) | collective-permute-done | bytes 98336 | tf_op jit(solution)/shard_map/ppermute | solution.py:25
  193.7 2.6 convolution_convert_fusion.1
  196.8 3.9 %collective-permute-start.9 = (bf16[16,16,1536]{2,1,0:T(8,128)(2,1)S(1)}, bf16[16,16,1536]{2,1,0:T(8,128)(2,1)S(1)}, u32[]{:S(2)}, u32[]{:S(2)}) collective-permute-start(bf16[16,16,1536]{2,1,0:T(8,128)(2,1)S(1)} %get-tuple-element.21), channel_id=1, source_target_pairs={{0,256},{1,257},{2,258},{3,259},{4,260},{5,261},{6,262},{7,263},{8... | collective-permute-start | bytes 2359304 | tf_op jit(solution)/shard_map/ppermute | solution.py:31
  200.7 12.9 %collective-permute-done.9 = bf16[16,16,1536]{2,1,0:T(8,128)(2,1)S(1)} collective-permute-done((bf16[16,16,1536]{2,1,0:T(8,128)(2,1)S(1)}, bf16[16,16,1536]{2,1,0:T(8,128)(2,1)S(1)}, u32[]{:S(2)}, u32[]{:S(2)}) %collective-permute-start.9) | collective-permute-done | bytes 786464 | tf_op jit(solution)/shard_map/ppermute | solution.py:31
  214.3 5.2 %fusion.15 = bf16[16,16,2304]{2,1,0:T(8,128)(2,1)S(1)} fusion(bf16[3072,1536]{1,0:T(8,128)(2,1)} %get-tuple-element.8, bf16[16,16,1536]{2,1,0:T(8,128)(2,1)S(1)} %get-tuple-element.19, f32[1536]{0:T(1024)S(1)} %get-tuple-element.15, f32[1536]{0:T(1024)S(1)} %get-tuple-element.10, f32[16,16]{1,0:T(8,128)S(1)} %add_rsqrt_fusion, ...), kind=kOutput, calls=%fused_computation.11 | convolution fusion | flops 1814888448 | bytes 9058304 | tf_op jit(solution)/shard_map/dot_general | solution.py:74
  219.6 4.2 %collective-permute-done.10 = bf16[4,16,2304]{2,1,0:T(8,128)(2,1)S(1)} collective-permute-done((bf16[4,16,2304]{2,1,0:T(8,128)(2,1)S(1)}, bf16[4,16,2304]{2,1,0:T(8,128)(2,1)S(1)}, u32[]{:S(2)}, u32[]{:S(2)}) %collective-permute-start.10) | collective-permute-done | bytes 294944 | tf_op jit(solution)/shard_map/ppermute | solution.py:25
  224.3 5.6 %collective-permute-start.11 = (bf16[16,4,2304]{2,1,0:T(4,128)(2,1)S(1)}, bf16[16,4,2304]{2,1,0:T(4,128)(2,1)S(1)}, u32[]{:S(2)}, u32[]{:S(2)}) collective-permute-start(bf16[16,4,2304]{2,1,0:T(4,128)(2,1)S(1)} %slice.192), channel_id=1, source_target_pairs={{0,15},{1,0},{2,1},{3,2},{4,3},{5,4},{6,5},{7,6},{8,7},{9,8},{10,9... | collective-permute-start | bytes 884744 | tf_op jit(solution)/shard_map/ppermute | solution.py:25
  229.9 13.7 %collective-permute-done.11 = bf16[16,4,2304]{2,1,0:T(4,128)(2,1)S(1)} collective-permute-done((bf16[16,4,2304]{2,1,0:T(4,128)(2,1)S(1)}, bf16[16,4,2304]{2,1,0:T(4,128)(2,1)S(1)}, u32[]{:S(2)}, u32[]{:S(2)}) %collective-permute-start.11) | collective-permute-done | bytes 294944 | tf_op jit(solution)/shard_map/ppermute | solution.py:25
  243.5 0.9 fusion.47
  244.9 1.2 fusion.41
  246.1 1.7 convolution_convert_fusion.3
  248.1 3.9 %collective-permute-done.12 = bf16[4,16,768]{2,1,0:T(8,128)(2,1)S(1)} collective-permute-done((bf16[4,16,768]{2,1,0:T(8,128)(2,1)S(1)}, bf16[4,16,768]{2,1,0:T(8,128)(2,1)S(1)}, u32[]{:S(2)}, u32[]{:S(2)}) %collective-permute-start.12) | collective-permute-done | bytes 98336 | tf_op jit(solution)/shard_map/ppermute | solution.py:25
  252.1 2.0 collective-permute-start.13
  254.1 1.1 copy.36
  255.3 9.0 %collective-permute-done.13 = bf16[16,4,768]{2,1,0:T(4,128)(2,1)S(1)} collective-permute-done((bf16[16,4,768]{2,1,0:T(4,128)(2,1)S(1)}, bf16[16,4,768]{2,1,0:T(4,128)(2,1)S(1)}, u32[]{:S(2)}, u32[]{:S(2)}) %collective-permute-start.13) | collective-permute-done | bytes 98336 | tf_op jit(solution)/shard_map/ppermute | solution.py:25
  264.2 1.8 convolution_convert_fusion
  266.1 1.3 fusion.54
  (90 shorter events, 8.9 us)
Async XLA Ops:
  0.0 3.8 %copy-start = (bf16[1,256,288]{1,2,0:T(8,128)(2,1)S(1)}, bf16[1,256,288]{1,2,0:T(8,128)(2,1)}, u32[]{:S(2)}) copy-start(bf16[1,256,288]{1,2,0:T(8,128)(2,1)} %param.11) | copy-start | bytes 442372
  0.0 4.1 %copy-start.11 = (bf16[1,768,96]{1,2,0:T(8,128)(2,1)S(1)}, bf16[1,768,96]{1,2,0:T(8,128)(2,1)}, u32[]{:S(2)}) copy-start(bf16[1,768,96]{1,2,0:T(8,128)(2,1)} %param.10) | copy-start | bytes 442372
  0.0 4.2 %copy-start.10 = (bf16[1,1536,144]{1,2,0:T(8,128)(2,1)S(1)}, bf16[1,1536,144]{1,2,0:T(8,128)(2,1)}, u32[]{:S(2)}) copy-start(bf16[1,1536,144]{1,2,0:T(8,128)(2,1)} %param.9) | copy-start | bytes 1327108
  3.6 52.6 %copy-start.1 = (bf16[2,16,16,1536]{3,2,1,0:T(8,128)(2,1)S(1)}, bf16[2,16,16,1536]{3,2,1,0:T(8,128)(2,1)}, u32[]{:S(2)}) copy-start(bf16[2,16,16,1536]{3,2,1,0:T(8,128)(2,1)} %param.6) | copy-start | bytes 4718596
  56.2 12.0 %copy-start.12 = (s32[1,2]{1,0:T(1,128)S(1)}, s32[1,2]{1,0:T(1,128)}, u32[]{:S(2)}) copy-start(s32[1,2]{1,0:T(1,128)} %param.8) | copy-start | bytes 28
  61.4 1.0 copy-start.7
  62.4 10.0 %collective-permute-start = (bf16[4,16,2304]{2,1,0:T(8,128)(2,1)S(1)}, bf16[4,16,2304]{2,1,0:T(8,128)(2,1)S(1)}, u32[]{:S(2)}, u32[]{:S(2)}) collective-permute-start(bf16[4,16,2304]{2,1,0:T(8,128)(2,1)S(1)} %slice.177), channel_id=1, source_target_pairs={{0,240},{16,0},{32,16},{48,32},{64,48},{80,64},{96,80},{112,96},{1... | collective-permute-start | bytes 884744 | tf_op jit(solution)/shard_map/ppermute | solution.py:25
  73.9 12.4 %collective-permute-start.1 = (bf16[16,4,2304]{2,1,0:T(4,128)(2,1)S(1)}, bf16[16,4,2304]{2,1,0:T(4,128)(2,1)S(1)}, u32[]{:S(2)}, u32[]{:S(2)}) collective-permute-start(bf16[16,4,2304]{2,1,0:T(4,128)(2,1)S(1)} %slice.178), channel_id=1, source_target_pairs={{0,15},{1,0},{2,1},{3,2},{4,3},{5,4},{6,5},{7,6},{8,7},{9,8},{10,9... | collective-permute-start | bytes 884744 | tf_op jit(solution)/shard_map/ppermute | solution.py:25
  88.4 4.1 %collective-permute-start.2 = (bf16[4,16,768]{2,1,0:T(8,128)(2,1)S(1)}, bf16[4,16,768]{2,1,0:T(8,128)(2,1)S(1)}, u32[]{:S(2)}, u32[]{:S(2)}) collective-permute-start(bf16[4,16,768]{2,1,0:T(8,128)(2,1)S(1)} %slice.182), channel_id=1, source_target_pairs={{0,16},{16,32},{32,48},{48,64},{64,80},{80,96},{96,112},{112,128},... | collective-permute-start | bytes 294920 | tf_op jit(solution)/shard_map/ppermute | solution.py:25
  92.6 17.8 %collective-permute-start.3 = (bf16[16,4,768]{2,1,0:T(4,128)(2,1)S(1)}, bf16[16,4,768]{2,1,0:T(4,128)(2,1)S(1)}, u32[]{:S(2)}, u32[]{:S(2)}) collective-permute-start(bf16[16,4,768]{2,1,0:T(4,128)(2,1)S(1)} %slice.183), channel_id=1, source_target_pairs={{0,1},{1,2},{2,3},{3,4},{4,5},{5,6},{6,7},{7,8},{8,9},{9,10},{10,1... | collective-permute-start | bytes 294920 | tf_op jit(solution)/shard_map/ppermute | solution.py:25
  113.5 26.6 %collective-permute-start.4 = (bf16[16,16,1536]{2,1,0:T(8,128)(2,1)S(1)}, bf16[16,16,1536]{2,1,0:T(8,128)(2,1)S(1)}, u32[]{:S(2)}, u32[]{:S(2)}) collective-permute-start(bf16[16,16,1536]{2,1,0:T(8,128)(2,1)S(1)} %get-tuple-element.25), channel_id=1, source_target_pairs={{0,256},{1,257},{2,258},{3,259},{4,260},{5,261},{6,262},{7,263},{8... | collective-permute-start | bytes 2359304 | tf_op jit(solution)/shard_map/ppermute | solution.py:31
  140.4 5.6 %copy-start.4 = (bf16[16,16,1536]{2,1,0:T(8,128)(2,1)}, bf16[16,16,1536]{2,1,0:T(8,128)(2,1)S(1)}, u32[]{:S(2)}) copy-start(bf16[16,16,1536]{2,1,0:T(8,128)(2,1)S(1)} %get-tuple-element.23) | copy-start | bytes 2359300
  146.0 4.3 %collective-permute-start.5 = (bf16[4,16,2304]{2,1,0:T(8,128)(2,1)S(1)}, bf16[4,16,2304]{2,1,0:T(8,128)(2,1)S(1)}, u32[]{:S(2)}, u32[]{:S(2)}) collective-permute-start(bf16[4,16,2304]{2,1,0:T(8,128)(2,1)S(1)} %slice.184), channel_id=1, source_target_pairs={{0,240},{16,0},{32,16},{48,32},{64,48},{80,64},{96,80},{112,96},{1... | collective-permute-start | bytes 884744 | tf_op jit(solution)/shard_map/ppermute | solution.py:25
  150.7 19.6 %collective-permute-start.6 = (bf16[16,4,2304]{2,1,0:T(4,128)(2,1)S(1)}, bf16[16,4,2304]{2,1,0:T(4,128)(2,1)S(1)}, u32[]{:S(2)}, u32[]{:S(2)}) collective-permute-start(bf16[16,4,2304]{2,1,0:T(4,128)(2,1)S(1)} %slice.185), channel_id=1, source_target_pairs={{0,15},{1,0},{2,1},{3,2},{4,3},{5,4},{6,5},{7,6},{8,7},{9,8},{10,9... | collective-permute-start | bytes 884744 | tf_op jit(solution)/shard_map/ppermute | solution.py:25
  177.4 4.1 %collective-permute-start.7 = (bf16[4,16,768]{2,1,0:T(8,128)(2,1)S(1)}, bf16[4,16,768]{2,1,0:T(8,128)(2,1)S(1)}, u32[]{:S(2)}, u32[]{:S(2)}) collective-permute-start(bf16[4,16,768]{2,1,0:T(8,128)(2,1)S(1)} %slice.189), channel_id=1, source_target_pairs={{0,16},{16,32},{32,48},{48,64},{64,80},{80,96},{96,112},{112,128},... | collective-permute-start | bytes 294920 | tf_op jit(solution)/shard_map/ppermute | solution.py:25
  181.5 0.7 copy-start.9
  182.3 11.4 %collective-permute-start.8 = (bf16[16,4,768]{2,1,0:T(4,128)(2,1)S(1)}, bf16[16,4,768]{2,1,0:T(4,128)(2,1)S(1)}, u32[]{:S(2)}, u32[]{:S(2)}) collective-permute-start(bf16[16,4,768]{2,1,0:T(4,128)(2,1)S(1)} %slice.190), channel_id=1, source_target_pairs={{0,1},{1,2},{2,3},{3,4},{4,5},{5,6},{6,7},{7,8},{8,9},{9,10},{10,1... | collective-permute-start | bytes 294920 | tf_op jit(solution)/shard_map/ppermute | solution.py:25
  184.2 12.1 %copy-start.5 = (bf16[16,16,1536]{2,1,0:T(8,128)(2,1)S(1)}, bf16[16,16,1536]{2,1,0:T(8,128)(2,1)}, u32[]{:S(2)}) copy-start(bf16[16,16,1536]{2,1,0:T(8,128)(2,1)} %copy-done.4) | copy-start | bytes 2359300
  196.8 16.8 %collective-permute-start.9 = (bf16[16,16,1536]{2,1,0:T(8,128)(2,1)S(1)}, bf16[16,16,1536]{2,1,0:T(8,128)(2,1)S(1)}, u32[]{:S(2)}, u32[]{:S(2)}) collective-permute-start(bf16[16,16,1536]{2,1,0:T(8,128)(2,1)S(1)} %get-tuple-element.21), channel_id=1, source_target_pairs={{0,256},{1,257},{2,258},{3,259},{4,260},{5,261},{6,262},{7,263},{8... | collective-permute-start | bytes 2359304 | tf_op jit(solution)/shard_map/ppermute | solution.py:31
  213.9 5.6 %copy-start.2 = (bf16[16,16,1536]{2,1,0:T(8,128)(2,1)}, bf16[16,16,1536]{2,1,0:T(8,128)(2,1)S(1)}, u32[]{:S(2)}) copy-start(bf16[16,16,1536]{2,1,0:T(8,128)(2,1)S(1)} %get-tuple-element.19) | copy-start | bytes 2359300
  219.5 4.3 %collective-permute-start.10 = (bf16[4,16,2304]{2,1,0:T(8,128)(2,1)S(1)}, bf16[4,16,2304]{2,1,0:T(8,128)(2,1)S(1)}, u32[]{:S(2)}, u32[]{:S(2)}) collective-permute-start(bf16[4,16,2304]{2,1,0:T(8,128)(2,1)S(1)} %slice.191), channel_id=1, source_target_pairs={{0,240},{16,0},{32,16},{48,32},{64,48},{80,64},{96,80},{112,96},{1... | collective-permute-start | bytes 884744 | tf_op jit(solution)/shard_map/ppermute | solution.py:25
  224.3 19.3 %collective-permute-start.11 = (bf16[16,4,2304]{2,1,0:T(4,128)(2,1)S(1)}, bf16[16,4,2304]{2,1,0:T(4,128)(2,1)S(1)}, u32[]{:S(2)}, u32[]{:S(2)}) collective-permute-start(bf16[16,4,2304]{2,1,0:T(4,128)(2,1)S(1)} %slice.192), channel_id=1, source_target_pairs={{0,15},{1,0},{2,1},{3,2},{4,3},{5,4},{6,5},{7,6},{8,7},{9,8},{10,9... | collective-permute-start | bytes 884744 | tf_op jit(solution)/shard_map/ppermute | solution.py:25
  247.9 4.1 %collective-permute-start.12 = (bf16[4,16,768]{2,1,0:T(8,128)(2,1)S(1)}, bf16[4,16,768]{2,1,0:T(8,128)(2,1)S(1)}, u32[]{:S(2)}, u32[]{:S(2)}) collective-permute-start(bf16[4,16,768]{2,1,0:T(8,128)(2,1)S(1)} %slice.196), channel_id=1, source_target_pairs={{0,16},{16,32},{32,48},{48,64},{64,80},{80,96},{96,112},{112,128},... | collective-permute-start | bytes 294920 | tf_op jit(solution)/shard_map/ppermute | solution.py:25
  252.0 2.1 copy-start.8
  252.1 12.1 %collective-permute-start.13 = (bf16[16,4,768]{2,1,0:T(4,128)(2,1)S(1)}, bf16[16,4,768]{2,1,0:T(4,128)(2,1)S(1)}, u32[]{:S(2)}, u32[]{:S(2)}) collective-permute-start(bf16[16,4,768]{2,1,0:T(4,128)(2,1)S(1)} %slice.197), channel_id=1, source_target_pairs={{0,1},{1,2},{2,3},{3,4},{4,5},{5,6},{6,7},{7,8},{8,9},{9,10},{10,1... | collective-permute-start | bytes 294920 | tf_op jit(solution)/shard_map/ppermute | solution.py:25
  254.1 10.1 %copy-start.6 = (bf16[16,2,48,768]{3,2,1,0:T(8,128)(2,1)S(1)}, bf16[16,2,48,768]{3,2,1,0:T(8,128)(2,1)}, u32[]{:S(2)}) copy-start(bf16[16,2,48,768]{3,2,1,0:T(8,128)(2,1)} %copy.20) | copy-start | bytes 7077892
  255.3 10.8 %copy-start.3 = (bf16[16,16,1536]{2,1,0:T(8,128)(2,1)S(1)}, bf16[16,16,1536]{2,1,0:T(8,128)(2,1)}, u32[]{:S(2)}) copy-start(bf16[16,16,1536]{2,1,0:T(8,128)(2,1)} %copy-done.2) | copy-start | bytes 2359300

commit v2 on v1

v2 whole, which is shorter than its diff:
```python
import math

import jax
import jax.numpy as jnp
from jax import lax
from jax.experimental import pallas as pl
from jax.experimental.pallas import tpu as pltpu
from jax.sharding import PartitionSpec as P

HEADS = 6
HD = 128
TEMB = 256
MB = 2
D = 1536
MESH = pl.DeviceIdType.MESH
UNIT = 48
EPSILON = 1e-06
BF16 = jnp.bfloat16
F32 = jnp.float32


def sinusoid(moments, entries):
    half_count = entries // 2
    frequency = jnp.exp(-math.log(10000.0) * jnp.arange(half_count, dtype=jnp.float32) / half_count)
    angles = moments.astype(jnp.float32)[:, None] * frequency[None, :]
    return jnp.concatenate([jnp.cos(angles), jnp.sin(angles)], axis=1)


def unit_row(w, q):
    last = q // 3
    return (144 * w + UNIT * q) * (1 - last) + (2304 + UNIT * w) * last


ORDER = (
    (0, -1), (0, 1), (-1, 0), (1, 0), (0, 2), (-1, -1), (1, -1), (-1, 1), (1, 1),
    (-1, 2), (1, 2), (2, 0), (2, -1), (2, 1), (2, 2),
)


def place():
    row, col = lax.axis_index("wrow"), lax.axis_index("wcol")
    return row, col, row // 2, row % 2, col // 4, col % 4


def gather_weights(comb, weights, sem_own, sem_send, sem_recv, sem_half):
    row, col, y, core, x, z = place()
    q = (y % 2) * 2 + core
    counter = [0]
    sends = []

    def unit(w, quarter, first=0, count=UNIT):
        start = pl.multiple_of(unit_row(w, quarter) + first, 16)
        return weights.at[pl.ds(start, count), :]

    def copy(w, quarter, target, slot, first=0, count=UNIT, recv=None):
        part = unit(w, quarter, first, count)
        return pltpu.make_async_remote_copy(
            src_ref=part,
            dst_ref=part,
            send_sem=sem_send.at[slot],
            recv_sem=sem_recv.at[w * 4 + quarter] if recv is None else recv,
            device_id=target,
            device_id_type=MESH,
        )

    def send(w, quarter, target, **kw):
        c = copy(w, quarter, target, counter[0], **kw)
        counter[0] += 1
        c.start()
        sends.append(c)

    def arrived(w, quarter, **kw):
        copy(w, quarter, {"wrow": row}, 0, **kw).wait_recv()

    def at_col(dx, dz):
        return {"wcol": ((x + dx + 4) % 4) * 4 + (z + dz + 4) % 4}

    partner = {"wrow": y * 2 + 1 - core}

    def number(dx, dz):
        return ((x + dx + 4) % 4) * 4 + (z + dz + 4) % 4

    def to_row(w):
        up = (w // 4 + w % 4) % 2
        return {"wrow": ((y + 7 + 2 * up) % 8) * 2 + core}

    own = []
    for quarter in range(4):
        c = pltpu.make_async_copy(
            comb.at[pl.ds(UNIT * quarter, UNIT), :], unit(col, quarter), sem_own.at[quarter]
        )
        c.start()
        own.append(c)

    def begin():
        for c in own:
            c.wait()
        for d in ((0, 1), (0, -1), (1, 0), (-1, 0)):
            send(col, q, at_col(*d))

    def plane():
        for dx, dz in ORDER:
            w = number(dx, dz)
            if (dx, dz) == (0, 2):
                arrived(w, q, first=0, count=32, recv=sem_half.at[0])
                arrived(w, q, first=32, count=16, recv=sem_half.at[1])
            else:
                arrived(w, q)
            if dx == 0:
                send(w, q, at_col(1, 0))
                send(w, q, at_col(-1, 0))
                if dz == -1:
                    send(w, q, at_col(0, 1), first=0, count=32, recv=sem_half.at[0])
                if dz == 1:
                    send(w, q, at_col(0, -1), first=32, count=16, recv=sem_half.at[1])
            if dx == -1 and dz in (0, -1):
                send(w, q, at_col(1, 0))
            if dx == 1 and dz in (1, 2):
                send(w, q, at_col(-1, 0))
            send(w, q, to_row(w))
            send(w, q, partner)

    def rows():
        qy = ((y + 1) % 2) * 2 + core
        for d in ORDER:
            arrived(number(*d), qy)
            send(number(*d), qy, partner)

    def sides():
        for d in ORDER:
            arrived(number(*d), (y % 2) * 2 + 1 - core)
        for d in ORDER:
            arrived(number(*d), ((y + 1) % 2) * 2 + 1 - core)

    def finish():
        for c in sends:
            c.wait_send()

    return begin, plane, rows, sides, finish


def iota(shape, axis):
    return lax.broadcasted_iota(jnp.int32, shape, axis)


def one_hot(index, width):
    return jnp.where(iota((index.shape[0], width), 1) == index, 1.0, 0.0).astype(BF16)


def pick(selector, rows):
    return jnp.dot(selector, rows, preferred_element_type=F32)


def times_rows(left, right):
    return lax.dot_general(left, right, (((1,), (1,)), ((), ())), preferred_element_type=F32)


def cell_slot(i, j):
    return jnp.where(j < 16, 16 * i + j, 304 + 4 * i + j)


def window_slot(u, v):
    slot = ((u >> 3) * 2 + (v >> 3)) * 64 + (u & 7) * 8 + (v & 7)
    inside = (u >= 0) & (u < 16) & (v >= 0) & (v < 16)
    return jnp.where(inside, slot, -1)


def block_kernel(
    comb, mod_own, states, shifts, out_ref,
    weights, out_rows, mods, modv, ext, pack, normed, triples, att, back, result,
    sem_own, sem_send, sem_recv, sem_half, sem_ms, sem_mr,
    sem_x, sem_hs, sem_hr, sem_bs, sem_br, sem_ps, sem_pr, sem_o,
):
    row, col, y, core, x, z = place()
    section = lax.axis_index("section")
    begin, plane, rows, sides, finish = gather_weights(
        comb, weights, sem_own, sem_send, sem_recv, sem_half
    )
    row_up, row_down = (row + 1) % 16, (row + 15) % 16
    col_up, col_down = (col + 1) % 16, (col + 15) % 16

    barrier = pltpu.get_barrier_semaphore()
    peers = [{"wcol": (col + k) % 16} for k in range(1, 16)]
    near = [
        {"wrow": y * 2 + 1 - core},
        {"wrow": ((y + 1) % 8) * 2 + core},
        {"wrow": ((y + 7) % 8) * 2 + core},
        {"wrow": (row + 2 * core + 15) % 16},
        {"wrow": row_up, "wcol": col_up},
        {"wrow": row_down, "wcol": col_down},
        {"section": 1 - section},
    ]
    for peer in peers + near:
        pl.semaphore_signal(barrier, inc=1, device_id=peer, device_id_type=MESH)
    pl.semaphore_wait(barrier, len(peers) + len(near))

    def remote(source, target, send_sem, recv_sem, device):
        return pltpu.make_async_remote_copy(
            src_ref=source,
            dst_ref=target,
            send_sem=send_sem,
            recv_sem=recv_sem,
            device_id=device,
            device_id_type=MESH,
        )

    begin()

    def own_state(b):
        return pltpu.make_async_copy(states.at[b], ext.at[b, pl.ds(0, 256), :], sem_x.at[b])

    def state_copy(b):
        return remote(
            result.at[b], ext.at[b, pl.ds(0, 256), :], sem_ps.at[b], sem_pr.at[b],
            {"section": 1 - section},
        )

    def borders(b):
        def piece(k, source, first, count, device):
            return remote(
                source, ext.at[b, pl.ds(first, count), :], sem_hs.at[3 * b + k],
                sem_hr.at[3 * b + k], device,
            )

        return (
            piece(0, ext.at[b, pl.ds(0, 64), :], 256, 64, {"wrow": row_down}),
            piece(1, pack.at[b], 320, 64, {"wcol": col_down}),
            piece(2, pack.at[b, pl.ds(0, 16), :], 384, 16, {"wrow": row_down, "wcol": col_down}),
        )

    def returns(b):
        def piece(k, at, first, count, device):
            return remote(
                back.at[b, pl.ds(at, count), :], att.at[b, pl.ds(first, count), :],
                sem_bs.at[3 * b + k], sem_br.at[3 * b + k], device,
            )

        return (
            piece(0, 0, 256, 64, {"wrow": row_up}),
            piece(1, 64, 320, 64, {"wcol": col_up}),
            piece(2, 128, 384, 16, {"wrow": row_up, "wcol": col_up}),
        )

    def send_borders(b):
        t = iota((64, 1), 0)
        selector = one_hot((t >> 2) * 16 + (t & 3), 256)
        pack[b] = pick(selector, ext[b, 0:256, :]).astype(BF16)
        for c in borders(b):
            c.start()

    @pl.when(section == 0)
    def _():
        for b in range(MB):
            own_state(b).start()
        for b in range(MB):
            own_state(b).wait()
            send_borders(b)

    mods[pl.ds(col, 1)] = mod_own[...][None]
    msends = []
    for k in range(1, 16):
        c = remote(mod_own, mods.at[col], sem_ms.at[k], sem_mr.at[col], peers[k - 1])
        c.start()
        msends.append(c)

    for b in range(MB):
        ext[b, 400:512, :] = jnp.zeros((112, D), BF16)
        att[b, 400:512, :] = jnp.zeros((112, HEADS * HD), BF16)

    plane()
    rows()
    for k in range(1, 16):
        other = (col + k) % 16
        remote(mod_own, mods.at[other], sem_ms.at[k], sem_mr.at[other], peers[k - 1]).wait_recv()

    pieces = mods[...].reshape(16 * 24, 128).astype(BF16)
    lane = iota((40, 128), 1) >> 5
    for b in range(MB):
        joined = jnp.zeros((40, 128), F32)
        for k in range(4):
            piece = iota((40, 1), 0) * 4 + k
            shard = (piece * 57) >> 9
            index = jnp.where(piece < 144, 24 * shard + 9 * b + piece - 9 * shard, -1)
            joined = jnp.where(lane == k, pick(one_hot(index, 384), pieces), joined)
        for t in range(36):
            modv[b, :, 128 * t : 128 * t + 128] = jnp.broadcast_to(joined[t : t + 1], (8, 128))

    sides()
    for w in range(16):
        packed = weights[2304 + UNIT * w : 2304 + UNIT * w + UNIT, :]
        out_rows[96 * w : 96 * w + 48, :] = packed[:, :768]
        out_rows[96 * w + 48 : 96 * w + 96, :] = packed[:, 768:]

    r, c = shifts[0, 0], shifts[0, 1]

    def compute(b):
        for copy in borders(b):
            copy.wait_recv()
        scale = 1.0 + modv[b, 0:1, D : 2 * D]
        shift = modv[b, 0:1, 0:D]

        def normalize(window, carry):
            t = iota((64, 1), 0)
            i = r + 8 * (window >> 1) + (t >> 3)
            j = c + 8 * (window & 1) + (t & 7)
            values = pick(one_hot(cell_slot(i, j), 512), ext[b])
            center = values - jnp.mean(values, axis=-1, keepdims=True)
            spread = jnp.mean(center * center, axis=-1, keepdims=True)
            center = center * lax.rsqrt(spread + EPSILON)
            normed[pl.ds(pl.multiple_of(64 * window, 64), 64), :] = (center * scale + shift).astype(
                BF16
            )
            return carry

        lax.fori_loop(0, 4, normalize, 0)

        def project(k, carry):
            at = pl.multiple_of(256 * k, 256)
            triples[:, pl.ds(at, 256)] = times_rows(
                normed[...], weights[pl.ds(at, 256), :]
            ).astype(BF16)
            return carry

        lax.fori_loop(0, 9, project, 0)

        same = (iota((128, 128), 0) >> 6) == (iota((128, 128), 1) >> 6)
        for head in range(HEADS):
            for pair in range(2):
                here = slice(128 * pair, 128 * pair + 128)
                query, key, value = (
                    triples[here, 768 * n + HD * head : 768 * n + HD * head + HD] for n in range(3)
                )
                scores = times_rows(query, key) * HD ** (-0.5)
                powers = jnp.where(same, jnp.exp(jnp.where(same, scores, 0.0)), 0.0)
                total = jnp.sum(powers, axis=-1, keepdims=True)
                chances = (powers / total).astype(BF16)
                att[b, here, HD * head : HD * head + HD] = pick(chances, value).astype(BF16)

        t = iota((144, 1), 0)
        s = t - 64
        q = t - 128
        i = jnp.where(t < 64, 16 + (t >> 4), jnp.where(t < 128, s >> 2, 16 + (q >> 2)))
        j = jnp.where(t < 64, t & 15, 16 + (t & 3))
        back[b] = pick(one_hot(window_slot(i - r, j - c), 256), att[b, 0:256, :]).astype(BF16)
        for copy in returns(b):
            copy.start()

    def complete(b):
        for copy in returns(b):
            copy.wait_recv()
        t = iota((256, 1), 0)
        i, j = t >> 4, t & 15
        index = jnp.where(
            i >= r,
            jnp.where(j >= c, window_slot(i - r, j - c), 320 + 4 * i + j),
            jnp.where(j >= c, 256 + 16 * i + j, 384 + 4 * i + j),
        )
        normed[:, 0:768] = pick(one_hot(index, 512), att[b]).astype(BF16)

        def project(k, carry):
            at = pl.multiple_of(256 * k, 256)
            projection = times_rows(normed[:, 0:768], out_rows[pl.ds(at, 256), :]).astype(BF16)
            gate = modv[b, 0:1, pl.ds(pl.multiple_of(2 * D + 256 * k, 256), 256)]
            kept = ext[b, 0:256, pl.ds(at, 256)].astype(F32)
            result[b, :, pl.ds(at, 256)] = (kept + gate * projection.astype(F32)).astype(BF16)
            return carry

        lax.fori_loop(0, 6, project, 0)
        pltpu.make_async_copy(result.at[b], out_ref.at[b], sem_o.at[b]).start()

        @pl.when(section == 0)
        def _():
            state_copy(b).start()

    def receive(b):
        @pl.when(section == 1)
        def _():
            state_copy(b).wait_recv()
            send_borders(b)

    receive(0)
    compute(0)

    @pl.when(section == 0)
    def _():
        compute(1)

    receive(1)
    complete(0)

    @pl.when(section == 1)
    def _():
        compute(1)

    complete(1)

    for b in range(MB):
        for copy in borders(b) + returns(b):
            copy.wait_send()
        pltpu.make_async_copy(result.at[b], out_ref.at[b], sem_o.at[b]).wait()

    @pl.when(section == 0)
    def _():
        for b in range(MB):
            state_copy(b).wait_send()

    finish()
    for copy in msends:
        copy.wait_send()


def blocks(comb, mod_own, states, shifts):
    dma = pltpu.SemaphoreType.DMA
    return pl.pallas_call(
        block_kernel,
        out_shape=jax.ShapeDtypeStruct((MB, 256, D), BF16),
        in_specs=[
            pl.BlockSpec(memory_space=pl.ANY),
            pl.BlockSpec(memory_space=pltpu.VMEM),
            pl.BlockSpec(memory_space=pl.ANY),
            pl.BlockSpec(memory_space=pltpu.SMEM),
        ],
        out_specs=pl.BlockSpec(memory_space=pl.ANY),
        scratch_shapes=[
            pltpu.VMEM((3072, D), BF16),
            pltpu.VMEM((D, 768), BF16),
            pltpu.VMEM((16, 24, 128), F32),
            pltpu.VMEM((MB, 8, 3 * D), F32),
            pltpu.VMEM((MB, 512, D), BF16),
            pltpu.VMEM((MB, 64, D), BF16),
            pltpu.VMEM((256, D), BF16),
            pltpu.VMEM((256, 2304), BF16),
            pltpu.VMEM((MB, 512, 768), BF16),
            pltpu.VMEM((MB, 144, 768), BF16),
            pltpu.VMEM((MB, 256, D), BF16),
            dma((4,)),
            dma((68,)),
            dma((64,)),
            dma((2,)),
            dma((16,)),
            dma((16,)),
            dma((MB,)),
            dma((3 * MB,)),
            dma((3 * MB,)),
            dma((3 * MB,)),
            dma((3 * MB,)),
            dma((MB,)),
            dma((MB,)),
            dma((MB,)),
        ],
        compiler_params=pltpu.CompilerParams(
            collective_id=0, has_side_effects=True, vmem_limit_bytes=56 << 20
        ),
        name="blocks",
    )(comb, mod_own, states, shifts)


def packed_modulation(mod_part):
    pieces = mod_part.astype(jnp.float32).reshape(MB * 9, 32)
    return jnp.pad(jnp.tile(pieces, (1, 4)), ((0, 6), (0, 0)))


def per_device(states, timesteps, shifts, qkv_weight, out_weight, mod_weight):
    embedding = jax.nn.silu(sinusoid(timesteps, TEMB)).astype(jnp.bfloat16)
    mod_part = jnp.dot(embedding, mod_weight[0], preferred_element_type=jnp.float32).astype(
        jnp.bfloat16
    )
    out_rows = out_weight[0].T
    comb = jnp.concatenate(
        [qkv_weight[0].T, jnp.concatenate([out_rows[:UNIT], out_rows[UNIT:]], axis=1)], axis=0
    )
    results = blocks(comb, packed_modulation(mod_part), states.reshape(MB, 256, D), shifts)
    return results.reshape((1,) + states.shape)


def solution(mesh):
    in_specs = (
        P(None, "wrow", "wcol", None),
        P(),
        P("section", None),
        P("section", None, "wcol"),
        P("section", None, "wcol"),
        P("section", None, "wcol"),
    )
    out_specs = P("section", None, "wrow", "wcol", None)
    return jax.shard_map(
        per_device, mesh=mesh, in_specs=in_specs, out_specs=out_specs, check_vma=False
    )
```

time: 268 us -> 158 us (0.59)
  the two profiles are of different devices: /device:TPU:56 before, /device:TPU:89 now
where the time goes in v2:
time: 158 us
  Pallas kernels  151 us (96%)
  local copies, waits for them, and re-layouts  4.5 us (3%)
  other arithmetic  2.68 us (2%)
    pallas_call x1, Pallas kernels, blocks(): pl.pallas_call(block_kernel, out_shape=jax.ShapeDtypeStruct((MB, 256, D),...  151 us

profile of v2, /device:TPU:89, one launch (start us, length us, event | category | flops | bytes accessed | tf_op | source)
XLA Modules:
  0.0 158.1 jit_solution(11542079060914519741)
XLA Ops:
  0.0 0.0 copy-start
  0.0 0.7 convert_element_type.12
  0.7 0.1 multiply_cosine_fusion
  0.8 0.1 copy-done
  0.9 0.1 fusion
  1.1 0.1 reshape.19
  1.2 0.1 tile.15
  1.3 0.6 pad.4.mod_own
  1.9 0.9 fusion.7
  2.8 1.9 %maximum_maximum_fusion.comb = bf16[192,1536]{1,0:T(8,128)(2,1)} fusion(bf16[48,768]{1,0:T(8,128)(2,1)S(1)} %get-tuple-element.6, bf16[48,768]{1,0:T(8,128)(2,1)S(1)} %get-tuple-element.5, bf16[144,1536]{1,0:T(8,128)(2,1)} %bitcast.13), kind=kLoop, calls=%fused_computation.2 | loop fusion | flops 1769472 | bytes 1179648 | tf_op jit(solution)/shard_map/concatenate | solution.py:469
  4.7 150.8 %blocks.1 = bf16[2,256,1536]{2,1,0:T(8,128)(2,1)} custom-call(bf16[192,1536]{1,0:T(8,128)(2,1)} %maximum_maximum_fusion.comb, f32[24,128]{1,0:T(8,128)} %pad.4.mod_own, bf16[2,256,1536]{2,1,0:T(8,128)(2,1)} %bitcast.12, s32[1,2]{1,0:T(1,128)} %shifts.1), custom_call_target="tpu_custom_call" | custom-call | tf_op jit(solution)/shard_map/blocks/pallas_call | solution.py:414
  155.5 2.7 %copy.8 = bf16[1,2,16,16,1536]{4,3,2,1,0:T(8,128)(2,1)} copy(bf16[1,2,16,16,1536]{4,3,2,1,0:T(8,128)(2,1)} %bitcast.11) | data formatting | bytes 3145728
  (2 shorter events, 0.0 us)
Async XLA Ops:
  0.0 0.9 copy-start

commit v3 on v2

--- a/solution.py
+++ b/solution.py
@@ -167,9 +167,11 @@
 
 def block_kernel(
     comb, mod_own, states, shifts, out_ref,
-    weights, out_rows, mods, modv, ext, pack, normed, triples, att, back, result,
+    weights, out_rows, first_packed, first_rows, mods, modv, gates, first_gates,
+    ext, pack, spread_in, spread_back, spread_own, spread_rim,
+    rolled, normed, triples, att, rim, back, handed, result,
     sem_own, sem_send, sem_recv, sem_half, sem_ms, sem_mr,
-    sem_x, sem_hs, sem_hr, sem_bs, sem_br, sem_ps, sem_pr, sem_o,
+    sem_x, sem_hs, sem_hr, sem_bs, sem_br, sem_ps, sem_pr, sem_o, sem_fs, sem_fr, sem_gs,
 ):
     row, col, y, core, x, z = place()
     section = lax.axis_index("section")
@@ -178,6 +180,7 @@
     )
     row_up, row_down = (row + 1) % 16, (row + 15) % 16
     col_up, col_down = (col + 1) % 16, (col + 15) % 16
+    col_before = x * 4 + (z + 3) % 4
 
     barrier = pltpu.get_barrier_semaphore()
     peers = [{"wcol": (col + k) % 16} for k in range(1, 16)]
@@ -189,6 +192,7 @@
         {"wrow": row_up, "wcol": col_up},
         {"wrow": row_down, "wcol": col_down},
         {"section": 1 - section},
+        {"section": 1 - section, "wcol": x * 4 + (z + 3 + 2 * section) % 4},
     ]
     for peer in peers + near:
         pl.semaphore_signal(barrier, inc=1, device_id=peer, device_id_type=MESH)
@@ -206,14 +210,38 @@
 
     begin()
 
-    def own_state(b):
-        return pltpu.make_async_copy(states.at[b], ext.at[b, pl.ds(0, 256), :], sem_x.at[b])
-
-    def state_copy(b):
+    def own_state(b, target):
+        return pltpu.make_async_copy(states.at[b], target, sem_x.at[b])
+
+    def hand_over(b):
         return remote(
-            result.at[b], ext.at[b, pl.ds(0, 256), :], sem_ps.at[b], sem_pr.at[b],
-            {"section": 1 - section},
-        )
+            handed.at[b], handed.at[b], sem_ps.at[b], sem_pr.at[b], {"section": 1 - section}
+        )
+
+    def hand_gates():
+        return remote(gates, first_gates, sem_gs.at[0], sem_gs.at[1], {"section": 1 - section})
+
+    def first_unit(slot, w, device):
+        part = pl.ds(pl.multiple_of(UNIT * w, 16), UNIT)
+        return remote(
+            weights.at[pl.ds(pl.multiple_of(2304 + UNIT * w, 16), UNIT), :],
+            first_packed.at[part, :], sem_fs.at[slot], sem_fr.at[w], device,
+        )
+
+    def relay_unit(slot, w):
+        part = pl.ds(pl.multiple_of(UNIT * w, 16), UNIT)
+        return remote(
+            first_packed.at[part, :], first_packed.at[part, :], sem_fs.at[slot], sem_fr.at[w],
+            {"wrow": y * 2 + 1 - core},
+        )
+
+    def first_sends():
+        ahead = [first_unit(k, 2 * k + core, {"section": 1 - section}) for k in range(4)]
+        behind = [
+            first_unit(k, 2 * k + core, {"section": 1 - section, "wcol": col_before})
+            for k in range(4, 8)
+        ]
+        return ahead + behind
 
     def borders(b):
         def piece(k, source, first, count, device):
@@ -229,16 +257,17 @@
         )
 
     def returns(b):
-        def piece(k, at, first, count, device):
+        def piece(k, at, count, device):
+            part = pl.ds(at, count)
             return remote(
-                back.at[b, pl.ds(at, count), :], att.at[b, pl.ds(first, count), :],
+                back.at[b, part, :], rim.at[b, part, :],
                 sem_bs.at[3 * b + k], sem_br.at[3 * b + k], device,
             )
 
         return (
-            piece(0, 0, 256, 64, {"wrow": row_up}),
-            piece(1, 64, 320, 64, {"wcol": col_up}),
-            piece(2, 128, 384, 16, {"wrow": row_up, "wcol": col_up}),
+            piece(0, 0, 64, {"wrow": row_up}),
+            piece(1, 64, 64, {"wcol": col_up}),
+            piece(2, 128, 16, {"wrow": row_up, "wcol": col_up}),
         )
 
     def send_borders(b):
@@ -251,10 +280,15 @@
     @pl.when(section == 0)
     def _():
         for b in range(MB):
-            own_state(b).start()
+            own_state(b, ext.at[b, pl.ds(0, 256), :]).start()
         for b in range(MB):
-            own_state(b).wait()
+            own_state(b, ext.at[b, pl.ds(0, 256), :]).wait()
             send_borders(b)
+
+    @pl.when(section == 1)
+    def _():
+        for b in range(MB):
+            own_state(b, result.at[b]).start()
 
     mods[pl.ds(col, 1)] = mod_own[...][None]
     msends = []
@@ -265,7 +299,27 @@
 
     for b in range(MB):
         ext[b, 400:512, :] = jnp.zeros((112, D), BF16)
-        att[b, 400:512, :] = jnp.zeros((112, HEADS * HD), BF16)
+        rim[b, 144:256, :] = jnp.zeros((112, HEADS * HD), BF16)
+
+    r, c = shifts[0, 0], shifts[0, 1]
+    t = iota((256, 1), 0)
+    i = r + 8 * (t >> 7) + ((t >> 3) & 7)
+    j = c + 8 * ((t >> 6) & 1) + (t & 7)
+    spread_in[...] = one_hot(cell_slot(i, j), 512)
+    i, j = t >> 4, t & 15
+    spread_own[...] = one_hot(window_slot(i - r, j - c), 256)
+    index = jnp.where(
+        i >= r,
+        jnp.where(j >= c, -1, 64 + 4 * i + j),
+        jnp.where(j >= c, 16 * i + j, 128 + 4 * i + j),
+    )
+    spread_rim[...] = one_hot(index, 256)
+    t = iota((144, 1), 0)
+    s = t - 64
+    q = t - 128
+    i = jnp.where(t < 64, 16 + (t >> 4), jnp.where(t < 128, s >> 2, 16 + (q >> 2)))
+    j = jnp.where(t < 64, t & 15, 16 + (t & 3))
+    spread_back[...] = one_hot(window_slot(i - r, j - c), 256)
 
     plane()
     rows()
@@ -275,6 +329,7 @@
 
     pieces = mods[...].reshape(16 * 24, 128).astype(BF16)
     lane = iota((40, 128), 1) >> 5
+    gates[...] = jnp.zeros((8, D), F32)
     for b in range(MB):
         joined = jnp.zeros((40, 128), F32)
         for k in range(4):
@@ -282,117 +337,110 @@
             shard = (piece * 57) >> 9
             index = jnp.where(piece < 144, 24 * shard + 9 * b + piece - 9 * shard, -1)
             joined = jnp.where(lane == k, pick(one_hot(index, 384), pieces), joined)
-        for t in range(36):
+        for t in range(24):
             modv[b, :, 128 * t : 128 * t + 128] = jnp.broadcast_to(joined[t : t + 1], (8, 128))
+        for t in range(12):
+            gates[b : b + 1, 128 * t : 128 * t + 128] = joined[24 + t : 25 + t]
 
     sides()
-    for w in range(16):
-        packed = weights[2304 + UNIT * w : 2304 + UNIT * w + UNIT, :]
-        out_rows[96 * w : 96 * w + 48, :] = packed[:, :768]
-        out_rows[96 * w + 48 : 96 * w + 96, :] = packed[:, 768:]
-
-    r, c = shifts[0, 0], shifts[0, 1]
+
+    @pl.when(section == 0)
+    def _():
+        hand_gates().start()
+        for copy in first_sends():
+            copy.start()
+
+    def unpack(source, base, target):
+        for w in range(16):
+            packed = source[base + UNIT * w : base + UNIT * w + UNIT, :]
+            target[96 * w : 96 * w + 48, :] = packed[:, :768]
+            target[96 * w + 48 : 96 * w + 96, :] = packed[:, 768:]
+
+    def add_projection(source, matrix, gate, kept, target):
+        for k in range(6):
+            here = slice(256 * k, 256 * k + 256)
+            projection = times_rows(source, matrix[here, :]).astype(BF16)
+            target[:, here] = (
+                kept[:, here].astype(F32) + gate[:, here] * projection.astype(F32)
+            ).astype(BF16)
 
     def compute(b):
         for copy in borders(b):
             copy.wait_recv()
+        for k in range(3):
+            here = slice(512 * k, 512 * k + 512)
+            rolled[:, here] = pick(spread_in[...], ext[b, :, here]).astype(BF16)
         scale = 1.0 + modv[b, 0:1, D : 2 * D]
         shift = modv[b, 0:1, 0:D]
-
-        def normalize(window, carry):
-            t = iota((64, 1), 0)
-            i = r + 8 * (window >> 1) + (t >> 3)
-            j = c + 8 * (window & 1) + (t & 7)
-            values = pick(one_hot(cell_slot(i, j), 512), ext[b])
+        for k in range(8):
+            here = slice(32 * k, 32 * k + 32)
+            values = rolled[here, :].astype(F32)
             center = values - jnp.mean(values, axis=-1, keepdims=True)
             spread = jnp.mean(center * center, axis=-1, keepdims=True)
             center = center * lax.rsqrt(spread + EPSILON)
-            normed[pl.ds(pl.multiple_of(64 * window, 64), 64), :] = (center * scale + shift).astype(
-                BF16
-            )
-            return carry
-
-        lax.fori_loop(0, 4, normalize, 0)
-
-        def project(k, carry):
-            at = pl.multiple_of(256 * k, 256)
-            triples[:, pl.ds(at, 256)] = times_rows(
-                normed[...], weights[pl.ds(at, 256), :]
-            ).astype(BF16)
-            return carry
-
-        lax.fori_loop(0, 9, project, 0)
+            normed[here, :] = (center * scale + shift).astype(BF16)
+        for k in range(3):
+            here = slice(768 * k, 768 * k + 768)
+            triples[here, :] = times_rows(weights[here, :], normed[...]).astype(BF16)
 
         same = (iota((128, 128), 0) >> 6) == (iota((128, 128), 1) >> 6)
         for head in range(HEADS):
             for pair in range(2):
                 here = slice(128 * pair, 128 * pair + 128)
                 query, key, value = (
-                    triples[here, 768 * n + HD * head : 768 * n + HD * head + HD] for n in range(3)
+                    triples[768 * n + HD * head : 768 * n + HD * head + HD, here] for n in range(3)
                 )
-                scores = times_rows(query, key) * HD ** (-0.5)
+                scores = lax.dot_general(
+                    key, query, (((0,), (0,)), ((), ())), preferred_element_type=F32
+                ) * HD ** (-0.5)
                 powers = jnp.where(same, jnp.exp(jnp.where(same, scores, 0.0)), 0.0)
-                total = jnp.sum(powers, axis=-1, keepdims=True)
+                total = jnp.sum(powers, axis=0, keepdims=True)
                 chances = (powers / total).astype(BF16)
-                att[b, here, HD * head : HD * head + HD] = pick(chances, value).astype(BF16)
-
-        t = iota((144, 1), 0)
-        s = t - 64
-        q = t - 128
-        i = jnp.where(t < 64, 16 + (t >> 4), jnp.where(t < 128, s >> 2, 16 + (q >> 2)))
-        j = jnp.where(t < 64, t & 15, 16 + (t & 3))
-        back[b] = pick(one_hot(window_slot(i - r, j - c), 256), att[b, 0:256, :]).astype(BF16)
+                att[b, HD * head : HD * head + HD, here] = pick(value, chances).astype(BF16)
+
+        back[b] = times_rows(spread_back[...], att[b]).astype(BF16)
         for copy in returns(b):
             copy.start()
 
     def complete(b):
         for copy in returns(b):
             copy.wait_recv()
-        t = iota((256, 1), 0)
-        i, j = t >> 4, t & 15
-        index = jnp.where(
-            i >= r,
-            jnp.where(j >= c, window_slot(i - r, j - c), 320 + 4 * i + j),
-            jnp.where(j >= c, 256 + 16 * i + j, 384 + 4 * i + j),
-        )
-        normed[:, 0:768] = pick(one_hot(index, 512), att[b]).astype(BF16)
-
-        def project(k, carry):
-            at = pl.multiple_of(256 * k, 256)
-            projection = times_rows(normed[:, 0:768], out_rows[pl.ds(at, 256), :]).astype(BF16)
-            gate = modv[b, 0:1, pl.ds(pl.multiple_of(2 * D + 256 * k, 256), 256)]
-            kept = ext[b, 0:256, pl.ds(at, 256)].astype(F32)
-            result[b, :, pl.ds(at, 256)] = (kept + gate * projection.astype(F32)).astype(BF16)
-            return carry
-
-        lax.fori_loop(0, 6, project, 0)
-        pltpu.make_async_copy(result.at[b], out_ref.at[b], sem_o.at[b]).start()
+        own = times_rows(spread_own[...], att[b])
+        handed[b] = (own + pick(spread_rim[...], rim[b])).astype(BF16)
 
         @pl.when(section == 0)
         def _():
-            state_copy(b).start()
-
-    def receive(b):
-        @pl.when(section == 1)
-        def _():
-            state_copy(b).wait_recv()
-            send_borders(b)
-
-    receive(0)
-    compute(0)
-
-    @pl.when(section == 0)
-    def _():
-        compute(1)
-
-    receive(1)
-    complete(0)
+            hand_over(b).start()
+
+        add_projection(
+            handed[b], out_rows, gates[b : b + 1, :], ext.at[b, pl.ds(0, 256), :], result.at[b]
+        )
+        pltpu.make_async_copy(result.at[b], out_ref.at[b], sem_o.at[b]).start()
+
+    unpack(weights, 2304, out_rows)
 
     @pl.when(section == 1)
     def _():
-        compute(1)
-
-    complete(1)
+        for k in range(8):
+            first_unit(k, 2 * k + core, {"section": 1 - section}).wait_recv()
+            relay_unit(k, 2 * k + core).start()
+        for k in range(8):
+            relay_unit(k, 2 * k + 1 - core).wait_recv()
+        unpack(first_packed, 0, first_rows)
+        hand_gates().wait_recv()
+        for b in range(MB):
+            own_state(b, result.at[b]).wait()
+            hand_over(b).wait_recv()
+            add_projection(
+                handed[b], first_rows, first_gates[b : b + 1, :], result.at[b],
+                ext.at[b, pl.ds(0, 256), :],
+            )
+            send_borders(b)
+
+    for b in range(MB):
+        compute(b)
+    for b in range(MB):
+        complete(b)
 
     for b in range(MB):
         for copy in borders(b) + returns(b):
@@ -402,7 +450,15 @@
     @pl.when(section == 0)
     def _():
         for b in range(MB):
-            state_copy(b).wait_send()
+            hand_over(b).wait_send()
+        hand_gates().wait_send()
+        for copy in first_sends():
+            copy.wait_send()
+
+    @pl.when(section == 1)
+    def _():
+        for k in range(8):
+            relay_unit(k, 2 * k + core).wait_send()
 
     finish()
     for copy in msends:
@@ -424,14 +480,25 @@
         scratch_shapes=[
             pltpu.VMEM((3072, D), BF16),
             pltpu.VMEM((D, 768), BF16),
+            pltpu.VMEM((768, D), BF16),
+            pltpu.VMEM((D, 768), BF16),
             pltpu.VMEM((16, 24, 128), F32),
-            pltpu.VMEM((MB, 8, 3 * D), F32),
+            pltpu.VMEM((MB, 8, 2 * D), F32),
+            pltpu.VMEM((8, D), F32),
+            pltpu.VMEM((8, D), F32),
             pltpu.VMEM((MB, 512, D), BF16),
             pltpu.VMEM((MB, 64, D), BF16),
+            pltpu.VMEM((256, 512), BF16),
+            pltpu.VMEM((144, 256), BF16),
+            pltpu.VMEM((256, 256), BF16),
+            pltpu.VMEM((256, 256), BF16),
             pltpu.VMEM((256, D), BF16),
-            pltpu.VMEM((256, 2304), BF16),
-            pltpu.VMEM((MB, 512, 768), BF16),
+            pltpu.VMEM((256, D), BF16),
+            pltpu.VMEM((2304, 256), BF16),
+            pltpu.VMEM((MB, 768, 256), BF16),
+            pltpu.VMEM((MB, 256, 768), BF16),
             pltpu.VMEM((MB, 144, 768), BF16),
+            pltpu.VMEM((MB, 256, 768), BF16),
             pltpu.VMEM((MB, 256, D), BF16),
             dma((4,)),
             dma((68,)),
@@ -447,9 +514,12 @@
             dma((MB,)),
             dma((MB,)),
             dma((MB,)),
+            dma((8,)),
+            dma((16,)),
+            dma((2,)),
         ],
         compiler_params=pltpu.CompilerParams(
-            collective_id=0, has_side_effects=True, vmem_limit_bytes=56 << 20
+            collective_id=0, has_side_effects=True, vmem_limit_bytes=60 << 20
         ),
         name="blocks",
     )(comb, mod_own, states, shifts)

time: 158 us -> 138 us (0.87)
  Pallas kernels: 151 us -> 130 us
    pallas_call x1, Pallas kernels: 151 us -> 130 us  [blocks(): pl.pallas_call(block_kernel, out_shape=jax.ShapeDtypeStruct((MB, 256, D),...]
where the time goes in v3:
time: 138 us; the launch traced here: 137 us
  Pallas kernels  130 us (94%)
  local copies, waits for them, and re-layouts  4.5 us (3%)
  other arithmetic  2.68 us (2%)
    pallas_call x1, Pallas kernels, blocks(): pl.pallas_call(block_kernel, out_shape=jax.ShapeDtypeStruct((MB, 256, D),...  130 us

profile of v3, /device:TPU:89, one launch (start us, length us, event | category | flops | bytes accessed | tf_op | source)
XLA Modules:
  0.0 137.4 jit_solution(15987998944484237492)
XLA Ops:
  0.0 0.0 copy-start
  0.0 0.7 convert_element_type.12
  0.7 0.1 multiply_cosine_fusion
  0.8 0.1 copy-done
  0.9 0.1 fusion
  1.1 0.1 reshape.19
  1.2 0.1 tile.15
  1.3 0.6 pad.4.mod_own
  1.9 0.9 fusion.7
  2.8 1.9 %maximum_maximum_fusion.comb = bf16[192,1536]{1,0:T(8,128)(2,1)} fusion(bf16[48,768]{1,0:T(8,128)(2,1)S(1)} %get-tuple-element.6, bf16[48,768]{1,0:T(8,128)(2,1)S(1)} %get-tuple-element.5, bf16[144,1536]{1,0:T(8,128)(2,1)} %bitcast.13), kind=kLoop, calls=%fused_computation.2 | loop fusion | flops 1769472 | bytes 1179648 | tf_op jit(solution)/shard_map/concatenate | solution.py:539
  4.7 130.1 %blocks.1 = bf16[2,256,1536]{2,1,0:T(8,128)(2,1)} custom-call(bf16[192,1536]{1,0:T(8,128)(2,1)} %maximum_maximum_fusion.comb, f32[24,128]{1,0:T(8,128)} %pad.4.mod_own, bf16[2,256,1536]{2,1,0:T(8,128)(2,1)} %bitcast.12, s32[1,2]{1,0:T(1,128)} %shifts.1), custom_call_target="tpu_custom_call" | custom-call | tf_op jit(solution)/shard_map/blocks/pallas_call | solution.py:470
  134.8 2.7 %copy.8 = bf16[1,2,16,16,1536]{4,3,2,1,0:T(8,128)(2,1)} copy(bf16[1,2,16,16,1536]{4,3,2,1,0:T(8,128)(2,1)} %bitcast.11) | data formatting | bytes 3145728
  (2 shorter events, 0.0 us)
Async XLA Ops:
  0.0 0.9 copy-start

commit v4 on v3

--- a/solution.py
+++ b/solution.py
@@ -42,87 +42,108 @@
     return row, col, row // 2, row % 2, col // 4, col % 4
 
 
-def gather_weights(comb, weights, sem_own, sem_send, sem_recv, sem_half):
+def gather_weights(qkv_t, out_t, weights, sem_own, sem_send, sem_piece, sem_unit):
     row, col, y, core, x, z = place()
     q = (y % 2) * 2 + core
-    counter = [0]
+    qy = ((y + 1) % 2) * 2 + core
     sends = []
 
-    def unit(w, quarter, first=0, count=UNIT):
-        start = pl.multiple_of(unit_row(w, quarter) + first, 16)
-        return weights.at[pl.ds(start, count), :]
-
-    def copy(w, quarter, target, slot, first=0, count=UNIT, recv=None):
-        part = unit(w, quarter, first, count)
+    def number(dx, dz):
+        return ((x + dx + 4) % 4) * 4 + (z + dz + 4) % 4
+
+    def at_col(dx, dz):
+        return {"wcol": number(dx, dz)}
+
+    def to_row(w):
+        up = (w // 4 + w % 4) % 2
+        return {"wrow": ((y + 7 + 2 * up) % 8) * 2 + core}
+
+    partner = {"wrow": y * 2 + 1 - core}
+
+    def copy(w, quarter, target, slot, piece=None):
+        first = 0 if piece is None else 16 * piece
+        count = UNIT if piece is None else 16
+        part = weights.at[pl.ds(pl.multiple_of(unit_row(w, quarter) + first, 16), count), :]
         return pltpu.make_async_remote_copy(
             src_ref=part,
             dst_ref=part,
             send_sem=sem_send.at[slot],
-            recv_sem=sem_recv.at[w * 4 + quarter] if recv is None else recv,
+            recv_sem=sem_unit.at[w * 4 + quarter] if piece is None else sem_piece.at[w * 3 + piece],
             device_id=target,
             device_id_type=MESH,
         )
 
-    def send(w, quarter, target, **kw):
-        c = copy(w, quarter, target, counter[0], **kw)
-        counter[0] += 1
+    def send(w, quarter, target, piece=None):
+        c = copy(w, quarter, target, len(sends), piece)
         c.start()
         sends.append(c)
 
-    def arrived(w, quarter, **kw):
-        copy(w, quarter, {"wrow": row}, 0, **kw).wait_recv()
-
-    def at_col(dx, dz):
-        return {"wcol": ((x + dx + 4) % 4) * 4 + (z + dz + 4) % 4}
-
-    partner = {"wrow": y * 2 + 1 - core}
-
-    def number(dx, dz):
-        return ((x + dx + 4) % 4) * 4 + (z + dz + 4) % 4
-
-    def to_row(w):
-        up = (w // 4 + w % 4) % 2
-        return {"wrow": ((y + 7 + 2 * up) % 8) * 2 + core}
-
-    own = []
-    for quarter in range(4):
-        c = pltpu.make_async_copy(
-            comb.at[pl.ds(UNIT * quarter, UNIT), :], unit(col, quarter), sem_own.at[quarter]
-        )
-        c.start()
-        own.append(c)
-
-    def begin():
+    def arrived(w, quarter, piece=None):
+        copy(w, quarter, partner, 0, piece).wait_recv()
+
+    def unit(w, quarter):
+        return weights.at[pl.ds(pl.multiple_of(unit_row(w, quarter), 16), UNIT), :]
+
+    own = [
+        pltpu.make_async_copy(qkv_t.at[pl.ds(UNIT * k, UNIT), :], unit(col, k), sem_own.at[k])
+        for k in range(3)
+    ] + [
+        pltpu.make_async_copy(
+            out_t.at[pl.ds(UNIT * k, UNIT), :], unit(col, 3).at[:, pl.ds(768 * k, 768)],
+            sem_own.at[3 + k],
+        )
+        for k in range(2)
+    ]
+
+    def load():
+        for c in own:
+            c.start()
         for c in own:
             c.wait()
-        for d in ((0, 1), (0, -1), (1, 0), (-1, 0)):
-            send(col, q, at_col(*d))
-
-    def plane():
-        for dx, dz in ORDER:
+
+    def begin():
+        for piece in range(3):
+            for d in ((0, 1), (0, -1), (1, 0), (-1, 0)):
+                send(col, q, at_col(*d), piece)
+        for d in ((1, 0), (-1, 0)):
+            send(col, qy, at_col(*d))
+
+    def plane(after_z):
+        def event(dx, dz, piece):
             w = number(dx, dz)
-            if (dx, dz) == (0, 2):
-                arrived(w, q, first=0, count=32, recv=sem_half.at[0])
-                arrived(w, q, first=32, count=16, recv=sem_half.at[1])
-            else:
-                arrived(w, q)
+            arrived(w, q, piece)
+            if dz == -1 and dx == 0 and piece < 2:
+                send(w, q, at_col(0, 1), piece)
+            if dz == 1 and dx == 0 and piece == 2:
+                send(w, q, at_col(0, -1), piece)
             if dx == 0:
-                send(w, q, at_col(1, 0))
-                send(w, q, at_col(-1, 0))
-                if dz == -1:
-                    send(w, q, at_col(0, 1), first=0, count=32, recv=sem_half.at[0])
-                if dz == 1:
-                    send(w, q, at_col(0, -1), first=32, count=16, recv=sem_half.at[1])
+                send(w, q, at_col(1, 0), piece)
+                send(w, q, at_col(-1, 0), piece)
             if dx == -1 and dz in (0, -1):
-                send(w, q, at_col(1, 0))
+                send(w, q, at_col(1, 0), piece)
             if dx == 1 and dz in (1, 2):
-                send(w, q, at_col(-1, 0))
-            send(w, q, to_row(w))
+                send(w, q, at_col(-1, 0), piece)
+
+        def whole(dx, dz):
+            w = number(dx, dz)
+            if dx == 0 or dz != 0 or dx == 2:
+                send(w, q, to_row(w))
             send(w, q, partner)
 
+        for group in (((0, -1), (0, 1), (-1, 0), (1, 0)), ((0, 2),)):
+            for piece in range(3):
+                for d in group:
+                    event(*d, piece)
+            for d in group:
+                whole(*d)
+        after_z()
+        for d in ORDER[5:]:
+            for piece in range(3):
+                event(*d, piece)
+            whole(*d)
+
     def rows():
-        qy = ((y + 1) % 2) * 2 + core
-        for d in ORDER:
+        for d in ((-1, 0), (1, 0), (0, -1), (0, 1)) + ORDER[4:]:
             arrived(number(*d), qy)
             send(number(*d), qy, partner)
 
@@ -136,7 +157,7 @@
         for c in sends:
             c.wait_send()
 
-    return begin, plane, rows, sides, finish
+    return load, begin, plane, rows, sides, finish
 
 
 def iota(shape, axis):
@@ -166,21 +187,21 @@
 
 
 def block_kernel(
-    comb, mod_own, states, shifts, out_ref,
+    qkv_t, out_t, mod_own, states, shifts, out_ref,
     weights, out_rows, first_packed, first_rows, mods, modv, gates, first_gates,
     ext, pack, spread_in, spread_back, spread_own, spread_rim,
     rolled, normed, triples, att, rim, back, handed, result,
-    sem_own, sem_send, sem_recv, sem_half, sem_ms, sem_mr,
+    sem_own, sem_send, sem_piece, sem_unit, sem_ms, sem_mr,
     sem_x, sem_hs, sem_hr, sem_bs, sem_br, sem_ps, sem_pr, sem_o, sem_fs, sem_fr, sem_gs,
+    sem_cs, sem_go,
 ):
     row, col, y, core, x, z = place()
     section = lax.axis_index("section")
-    begin, plane, rows, sides, finish = gather_weights(
-        comb, weights, sem_own, sem_send, sem_recv, sem_half
+    load, begin, plane, rows, sides, finish = gather_weights(
+        qkv_t, out_t, weights, sem_own, sem_send, sem_piece, sem_unit
     )
     row_up, row_down = (row + 1) % 16, (row + 15) % 16
     col_up, col_down = (col + 1) % 16, (col + 15) % 16
-    col_before = x * 4 + (z + 3) % 4
 
     barrier = pltpu.get_barrier_semaphore()
     peers = [{"wcol": (col + k) % 16} for k in range(1, 16)]
@@ -192,10 +213,16 @@
         {"wrow": row_up, "wcol": col_up},
         {"wrow": row_down, "wcol": col_down},
         {"section": 1 - section},
-        {"section": 1 - section, "wcol": x * 4 + (z + 3 + 2 * section) % 4},
+        {"section": 1 - section, "wcol": (col + 15 + 2 * section) % 16},
+        {
+            "section": 1 - section,
+            "wrow": (row + 15 + 2 * section) % 16,
+            "wcol": (col + 15 + 2 * section) % 16,
+        },
     ]
     for peer in peers + near:
         pl.semaphore_signal(barrier, inc=1, device_id=peer, device_id_type=MESH)
+    load()
     pl.semaphore_wait(barrier, len(peers) + len(near))
 
     def remote(source, target, send_sem, recv_sem, device):
@@ -208,8 +235,6 @@
             device_id_type=MESH,
         )
 
-    begin()
-
     def own_state(b, target):
         return pltpu.make_async_copy(states.at[b], target, sem_x.at[b])
 
@@ -238,7 +263,7 @@
     def first_sends():
         ahead = [first_unit(k, 2 * k + core, {"section": 1 - section}) for k in range(4)]
         behind = [
-            first_unit(k, 2 * k + core, {"section": 1 - section, "wcol": col_before})
+            first_unit(k, 2 * k + core, {"section": 1 - section, "wcol": col_down})
             for k in range(4, 8)
         ]
         return ahead + behind
@@ -270,25 +295,43 @@
             piece(2, 128, 16, {"wrow": row_up, "wcol": col_up}),
         )
 
-    def send_borders(b):
+    def cross_borders(b):
+        def piece(k, count, device):
+            return remote(
+                pack.at[b, pl.ds(0, count), :], ext.at[b, pl.ds(256 + 64 * k, count), :],
+                sem_cs.at[2 * b + k - 1], sem_hr.at[3 * b + k], device,
+            )
+
+        return (
+            piece(1, 64, {"section": 1 - section, "wcol": col_down}),
+            piece(2, 16, {"section": 1 - section, "wrow": row_down, "wcol": col_down}),
+        )
+
+    def pack_columns(b, source):
         t = iota((64, 1), 0)
         selector = one_hot((t >> 2) * 16 + (t & 3), 256)
-        pack[b] = pick(selector, ext[b, 0:256, :]).astype(BF16)
-        for c in borders(b):
-            c.start()
+        pack[b] = pick(selector, source).astype(BF16)
 
     @pl.when(section == 0)
     def _():
         for b in range(MB):
             own_state(b, ext.at[b, pl.ds(0, 256), :]).start()
-        for b in range(MB):
-            own_state(b, ext.at[b, pl.ds(0, 256), :]).wait()
-            send_borders(b)
 
     @pl.when(section == 1)
     def _():
         for b in range(MB):
             own_state(b, result.at[b]).start()
+
+    def go():
+        pl.semaphore_signal(
+            sem_go, inc=1, device_id={"section": 1 - section}, device_id_type=MESH
+        )
+
+    @pl.when(section == 1)
+    def _():
+        pl.semaphore_wait(sem_go, 1)
+
+    begin()
 
     mods[pl.ds(col, 1)] = mod_own[...][None]
     msends = []
@@ -321,7 +364,17 @@
     j = jnp.where(t < 64, t & 15, 16 + (t & 3))
     spread_back[...] = one_hot(window_slot(i - r, j - c), 256)
 
-    plane()
+    def after_z():
+        @pl.when(section == 0)
+        def _():
+            go()
+            for b in range(MB):
+                own_state(b, ext.at[b, pl.ds(0, 256), :]).wait()
+                pack_columns(b, ext[b, 0:256, :])
+                for copy in borders(b):
+                    copy.start()
+
+    plane(after_z)
     rows()
     for k in range(1, 16):
         other = (col + k) % 16
@@ -342,14 +395,6 @@
         for t in range(12):
             gates[b : b + 1, 128 * t : 128 * t + 128] = joined[24 + t : 25 + t]
 
-    sides()
-
-    @pl.when(section == 0)
-    def _():
-        hand_gates().start()
-        for copy in first_sends():
-            copy.start()
-
     def unpack(source, base, target):
         for w in range(16):
             packed = source[base + UNIT * w : base + UNIT * w + UNIT, :]
@@ -364,7 +409,7 @@
                 kept[:, here].astype(F32) + gate[:, here] * projection.astype(F32)
             ).astype(BF16)
 
-    def compute(b):
+    def prepare(b):
         for copy in borders(b):
             copy.wait_recv()
         for k in range(3):
@@ -378,10 +423,11 @@
             center = values - jnp.mean(values, axis=-1, keepdims=True)
             spread = jnp.mean(center * center, axis=-1, keepdims=True)
             center = center * lax.rsqrt(spread + EPSILON)
-            normed[here, :] = (center * scale + shift).astype(BF16)
+            normed[b, here, :] = (center * scale + shift).astype(BF16)
+    def compute(b):
         for k in range(3):
             here = slice(768 * k, 768 * k + 768)
-            triples[here, :] = times_rows(weights[here, :], normed[...]).astype(BF16)
+            triples[here, :] = times_rows(weights[here, :], normed[b]).astype(BF16)
 
         same = (iota((128, 128), 0) >> 6) == (iota((128, 128), 1) >> 6)
         for head in range(HEADS):
@@ -415,9 +461,29 @@
         add_projection(
             handed[b], out_rows, gates[b : b + 1, :], ext.at[b, pl.ds(0, 256), :], result.at[b]
         )
+
+        @pl.when(section == 0)
+        def _():
+            for copy in borders(b)[1:]:
+                copy.wait_send()
+            pack_columns(b, result[b])
+            for copy in cross_borders(b):
+                copy.start()
+
         pltpu.make_async_copy(result.at[b], out_ref.at[b], sem_o.at[b]).start()
 
-    unpack(weights, 2304, out_rows)
+    @pl.when(section == 0)
+    def _():
+        for b in range(MB):
+            prepare(b)
+
+    sides()
+
+    @pl.when(section == 0)
+    def _():
+        hand_gates().start()
+        for copy in first_sends():
+            copy.start()
 
     @pl.when(section == 1)
     def _():
@@ -435,15 +501,19 @@
                 handed[b], first_rows, first_gates[b : b + 1, :], result.at[b],
                 ext.at[b, pl.ds(0, 256), :],
             )
-            send_borders(b)
+            borders(b)[0].start()
+        for b in range(MB):
+            prepare(b)
 
     for b in range(MB):
         compute(b)
+    unpack(weights, 2304, out_rows)
     for b in range(MB):
         complete(b)
 
     for b in range(MB):
-        for copy in borders(b) + returns(b):
+        borders(b)[0].wait_send()
+        for copy in returns(b):
             copy.wait_send()
         pltpu.make_async_copy(result.at[b], out_ref.at[b], sem_o.at[b]).wait()
 
@@ -451,6 +521,8 @@
     def _():
         for b in range(MB):
             hand_over(b).wait_send()
+            for copy in cross_borders(b):
+                copy.wait_send()
         hand_gates().wait_send()
         for copy in first_sends():
             copy.wait_send()
@@ -465,12 +537,13 @@
         copy.wait_send()
 
 
-def blocks(comb, mod_own, states, shifts):
+def blocks(qkv_t, out_t, mod_own, states, shifts):
     dma = pltpu.SemaphoreType.DMA
     return pl.pallas_call(
         block_kernel,
         out_shape=jax.ShapeDtypeStruct((MB, 256, D), BF16),
         in_specs=[
+            pl.BlockSpec(memory_space=pl.ANY),
             pl.BlockSpec(memory_space=pl.ANY),
             pl.BlockSpec(memory_space=pltpu.VMEM),
             pl.BlockSpec(memory_space=pl.ANY),
@@ -493,17 +566,17 @@
             pltpu.VMEM((256, 256), BF16),
             pltpu.VMEM((256, 256), BF16),
             pltpu.VMEM((256, D), BF16),
-            pltpu.VMEM((256, D), BF16),
+            pltpu.VMEM((MB, 256, D), BF16),
             pltpu.VMEM((2304, 256), BF16),
             pltpu.VMEM((MB, 768, 256), BF16),
             pltpu.VMEM((MB, 256, 768), BF16),
             pltpu.VMEM((MB, 144, 768), BF16),
             pltpu.VMEM((MB, 256, 768), BF16),
             pltpu.VMEM((MB, 256, D), BF16),
-            dma((4,)),
-            dma((68,)),
+            dma((5,)),
+            dma((96,)),
+            dma((48,)),
             dma((64,)),
-            dma((2,)),
             dma((16,)),
             dma((16,)),
             dma((MB,)),
@@ -517,12 +590,14 @@
             dma((8,)),
             dma((16,)),
             dma((2,)),
+            dma((2 * MB,)),
+            pltpu.SemaphoreType.REGULAR,
         ],
         compiler_params=pltpu.CompilerParams(
             collective_id=0, has_side_effects=True, vmem_limit_bytes=60 << 20
         ),
         name="blocks",
-    )(comb, mod_own, states, shifts)
+    )(qkv_t, out_t, mod_own, states, shifts)
 
 
 def packed_modulation(mod_part):
@@ -535,11 +610,9 @@
     mod_part = jnp.dot(embedding, mod_weight[0], preferred_element_type=jnp.float32).astype(
         jnp.bfloat16
     )
-    out_rows = out_weight[0].T
-    comb = jnp.concatenate(
-        [qkv_weight[0].T, jnp.concatenate([out_rows[:UNIT], out_rows[UNIT:]], axis=1)], axis=0
+    results = blocks(
+        qkv_weight[0].T, out_weight[0].T, packed_modulation(mod_part), states.reshape(MB, 256, D), shifts
     )
-    results = blocks(comb, packed_modulation(mod_part), states.reshape(MB, 256, D), shifts)
     return results.reshape((1,) + states.shape)
 
 

time: 138 us -> 125 us (0.906); the launches traced: 137 us -> 123 us
  Pallas kernels: 130 us -> 118 us
  other arithmetic: 2.68 us -> 0.81 us
    pallas_call x1, Pallas kernels: 130 us -> 118 us  [blocks(): pl.pallas_call(block_kernel, out_shape=jax.ShapeDtypeStruct((MB, 256, D),...]
    concatenate x1 -> x0, other arithmetic: 1.87 us -> none  [per_device(): jnp.concatenate([qkv_weight[0].T, jnp.concatenate([out_rows[:UNIT], out_r...]
where the time goes in v4:
time: 125 us; the launch traced here: 123 us
  Pallas kernels  118 us (94%)
  local copies, waits for them, and re-layouts  3.58 us (3%)
    pallas_call x1, Pallas kernels, blocks(): pl.pallas_call(block_kernel, out_shape=jax.ShapeDtypeStruct((MB, 256, D),...  118 us
    unnamed x3, local copies, waits for them, and re-layouts  2.76 us

profile of v4, /device:TPU:89, one launch (start us, length us, event | category | flops | bytes accessed | tf_op | source)
XLA Modules:
  0.0 122.8 jit_solution(14988850347154055760)
XLA Ops:
  0.0 0.0 copy-start
  0.0 0.7 convert_element_type.12
  0.7 0.1 multiply_cosine_fusion
  0.8 0.1 copy-done
  0.9 0.1 fusion
  1.1 0.1 reshape.19
  1.2 0.1 tile.15
  1.3 0.6 pad.4.mod_own
  1.9 118.2 %blocks.1 = bf16[2,256,1536]{2,1,0:T(8,128)(2,1)} custom-call(bf16[144,1536]{1,0:T(8,128)(2,1)} %bitcast.13, bf16[96,768]{1,0:T(8,128)(2,1)} %bitcast.14, f32[24,128]{1,0:T(8,128)} %pad.4.mod_own, bf16[2,256,1536]{2,1,0:T(8,128)(2,1)} %bitcast.12, s32[1,2]{1,0:T(1,128)} %shifts.1), custom_call_target="tpu_custom_call" | custom-call | tf_op jit(solution)/shard_map/blocks/pallas_call | solution.py:542
  120.1 2.7 %copy.8 = bf16[1,2,16,16,1536]{4,3,2,1,0:T(8,128)(2,1)} copy(bf16[1,2,16,16,1536]{4,3,2,1,0:T(8,128)(2,1)} %bitcast.11) | data formatting | bytes 3145728
  (2 shorter events, 0.0 us)
Async XLA Ops:
  0.0 0.9 copy-start

commit v5 on v4

--- a/solution.py
+++ b/solution.py
@@ -54,8 +54,10 @@
     def at_col(dx, dz):
         return {"wcol": number(dx, dz)}
 
-    def to_row(w):
-        up = (w // 4 + w % 4) % 2
+    crossing = [d for d in ORDER if d not in ((-1, 0), (1, 0))]
+
+    def to_row(d):
+        up = crossing.index(d) % 2
         return {"wrow": ((y + 7 + 2 * up) % 8) * 2 + core}
 
     partner = {"wrow": y * 2 + 1 - core}
@@ -126,8 +128,8 @@
 
         def whole(dx, dz):
             w = number(dx, dz)
-            if dx == 0 or dz != 0 or dx == 2:
-                send(w, q, to_row(w))
+            if (dx, dz) in crossing:
+                send(w, q, to_row((dx, dz)))
             send(w, q, partner)
 
         for group in (((0, -1), (0, 1), (-1, 0), (1, 0)), ((0, 2),)):
@@ -253,20 +255,49 @@
             first_packed.at[part, :], sem_fs.at[slot], sem_fr.at[w], device,
         )
 
-    def relay_unit(slot, w):
+    def relay_unit(slot, w, device):
         part = pl.ds(pl.multiple_of(UNIT * w, 16), UNIT)
         return remote(
             first_packed.at[part, :], first_packed.at[part, :], sem_fs.at[slot], sem_fr.at[w],
-            {"wrow": y * 2 + 1 - core},
-        )
+            device,
+        )
+
+    def first_own(k):
+        return 4 * k + 2 * core + y % 2
+
+    def first_near(k):
+        return 4 * k + 2 * core + (y + 1) % 2
+
+    behind = {"section": 1 - section, "wcol": col_down}
+    partner = {"wrow": y * 2 + 1 - core}
 
     def first_sends():
-        ahead = [first_unit(k, 2 * k + core, {"section": 1 - section}) for k in range(4)]
-        behind = [
-            first_unit(k, 2 * k + core, {"section": 1 - section, "wcol": col_down})
-            for k in range(4, 8)
+        return [first_unit(k, first_own(k), behind) for k in range(4)]
+
+    def first_rows_sends():
+        return [
+            relay_unit(k, first_own(k), {"wrow": ((y + (1 if k < 2 else 7)) % 8) * 2 + core})
+            for k in range(4)
         ]
-        return ahead + behind
+
+    def first_relays():
+        return [relay_unit(4 + k, first_own(k), partner) for k in range(4)] + [
+            relay_unit(8 + k, first_near(k), partner) for k in range(4)
+        ]
+
+    def receive_first():
+        swaps, relays = first_rows_sends(), first_relays()
+        for k in range(4):
+            first_unit(k, first_own(k), behind).wait_recv()
+            swaps[k].start()
+            relays[k].start()
+        for k in range(4):
+            first_unit(k, first_near(k), behind).wait_recv()
+            relays[4 + k].start()
+        for k in range(4):
+            for cls in range(2):
+                first_unit(k, 4 * k + 2 * (1 - core) + cls, behind).wait_recv()
+        unpack(first_packed, 0, first_rows)
 
     def borders(b):
         def piece(k, source, first, count, device):
@@ -334,11 +365,10 @@
     begin()
 
     mods[pl.ds(col, 1)] = mod_own[...][None]
-    msends = []
-    for k in range(1, 16):
-        c = remote(mod_own, mods.at[col], sem_ms.at[k], sem_mr.at[col], peers[k - 1])
-        c.start()
-        msends.append(c)
+    msends = [
+        remote(mod_own, mods.at[col], sem_ms.at[k], sem_mr.at[col], peers[k - 1])
+        for k in range(1, 16)
+    ]
 
     for b in range(MB):
         ext[b, 400:512, :] = jnp.zeros((112, D), BF16)
@@ -365,6 +395,9 @@
     spread_back[...] = one_hot(window_slot(i - r, j - c), 256)
 
     def after_z():
+        for copy in msends:
+            copy.start()
+
         @pl.when(section == 0)
         def _():
             go()
@@ -380,16 +413,19 @@
         other = (col + k) % 16
         remote(mod_own, mods.at[other], sem_ms.at[k], sem_mr.at[other], peers[k - 1]).wait_recv()
 
-    pieces = mods[...].reshape(16 * 24, 128).astype(BF16)
+    pieces = mods[...].reshape(256, 128)
+    turned = jnp.concatenate([pieces[:, 64:], pieces[:, :64]], axis=1)
+    low = iota((256, 128), 1) < 64
     lane = iota((40, 128), 1) >> 5
     gates[...] = jnp.zeros((8, D), F32)
     for b in range(MB):
         joined = jnp.zeros((40, 128), F32)
+        whole = jnp.where(low, pieces, turned) if b == 0 else jnp.where(low, turned, pieces)
         for k in range(4):
             piece = iota((40, 1), 0) * 4 + k
             shard = (piece * 57) >> 9
-            index = jnp.where(piece < 144, 24 * shard + 9 * b + piece - 9 * shard, -1)
-            joined = jnp.where(lane == k, pick(one_hot(index, 384), pieces), joined)
+            index = jnp.where(piece < 144, 16 * shard + piece - 9 * shard, -1)
+            joined = jnp.where(lane == k, pick(one_hot(index, 256), whole), joined)
         for t in range(24):
             modv[b, :, 128 * t : 128 * t + 128] = jnp.broadcast_to(joined[t : t + 1], (8, 128))
         for t in range(12):
@@ -448,7 +484,7 @@
         for copy in returns(b):
             copy.start()
 
-    def complete(b):
+    def restore(b):
         for copy in returns(b):
             copy.wait_recv()
         own = times_rows(spread_own[...], att[b])
@@ -458,6 +494,7 @@
         def _():
             hand_over(b).start()
 
+    def project(b):
         add_projection(
             handed[b], out_rows, gates[b : b + 1, :], ext.at[b, pl.ds(0, 256), :], result.at[b]
         )
@@ -485,31 +522,40 @@
         for copy in first_sends():
             copy.start()
 
+    def next_state(b):
+        own_state(b, result.at[b]).wait()
+        hand_over(b).wait_recv()
+        add_projection(
+            handed[b], first_rows, first_gates[b : b + 1, :], result.at[b],
+            ext.at[b, pl.ds(0, 256), :],
+        )
+        borders(b)[0].start()
+
+    @pl.when(section == 0)
+    def _():
+        compute(0)
+        compute(1)
+        restore(0)
+        unpack(weights, 2304, out_rows)
+        project(0)
+        restore(1)
+        project(1)
+
     @pl.when(section == 1)
     def _():
-        for k in range(8):
-            first_unit(k, 2 * k + core, {"section": 1 - section}).wait_recv()
-            relay_unit(k, 2 * k + core).start()
-        for k in range(8):
-            relay_unit(k, 2 * k + 1 - core).wait_recv()
-        unpack(first_packed, 0, first_rows)
+        receive_first()
+        unpack(weights, 2304, out_rows)
         hand_gates().wait_recv()
-        for b in range(MB):
-            own_state(b, result.at[b]).wait()
-            hand_over(b).wait_recv()
-            add_projection(
-                handed[b], first_rows, first_gates[b : b + 1, :], result.at[b],
-                ext.at[b, pl.ds(0, 256), :],
-            )
-            borders(b)[0].start()
-        for b in range(MB):
-            prepare(b)
-
-    for b in range(MB):
-        compute(b)
-    unpack(weights, 2304, out_rows)
-    for b in range(MB):
-        complete(b)
+        next_state(0)
+        prepare(0)
+        compute(0)
+        next_state(1)
+        restore(0)
+        project(0)
+        prepare(1)
+        compute(1)
+        restore(1)
+        project(1)
 
     for b in range(MB):
         borders(b)[0].wait_send()
@@ -529,8 +575,8 @@
 
     @pl.when(section == 1)
     def _():
-        for k in range(8):
-            relay_unit(k, 2 * k + core).wait_send()
+        for copy in first_rows_sends() + first_relays():
+            copy.wait_send()
 
     finish()
     for copy in msends:
@@ -555,7 +601,7 @@
             pltpu.VMEM((D, 768), BF16),
             pltpu.VMEM((768, D), BF16),
             pltpu.VMEM((D, 768), BF16),
-            pltpu.VMEM((16, 24, 128), F32),
+            pltpu.VMEM((16, 16, 128), BF16),
             pltpu.VMEM((MB, 8, 2 * D), F32),
             pltpu.VMEM((8, D), F32),
             pltpu.VMEM((8, D), F32),
@@ -587,7 +633,7 @@
             dma((MB,)),
             dma((MB,)),
             dma((MB,)),
-            dma((8,)),
+            dma((12,)),
             dma((16,)),
             dma((2,)),
             dma((2 * MB,)),
@@ -601,8 +647,9 @@
 
 
 def packed_modulation(mod_part):
-    pieces = mod_part.astype(jnp.float32).reshape(MB * 9, 32)
-    return jnp.pad(jnp.tile(pieces, (1, 4)), ((0, 6), (0, 0)))
+    pieces = mod_part.reshape(MB, 9, 1, 32)
+    doubled = jnp.concatenate([pieces, pieces], axis=2).transpose(1, 0, 2, 3)
+    return jnp.pad(doubled.reshape(9, 128), ((0, 7), (0, 0)))
 
 
 def per_device(states, timesteps, shifts, qkv_weight, out_weight, mod_weight):

time: 125 us -> 121 us (0.968)
  the two profiles are of different devices: /device:TPU:89 before, /device:TPU:65 now
where the time goes in v5:
time: 121 us
  Pallas kernels  116 us (96%)
  local copies, waits for them, and re-layouts  3.55 us (3%)
    pallas_call x1, Pallas kernels, blocks(): pl.pallas_call(block_kernel, out_shape=jax.ShapeDtypeStruct((MB, 256, D),...  116 us
    unnamed x3, local copies, waits for them, and re-layouts  2.76 us

profile of v5, /device:TPU:65, one launch (start us, length us, event | category | flops | bytes accessed | tf_op | source)
XLA Modules:
  0.0 121.1 jit_solution(10489989653901065615)
XLA Ops:
  0.0 0.0 copy-start
  0.0 0.7 convert_element_type.11
  0.7 0.1 multiply_cosine_fusion
  0.8 0.1 copy-done
  0.9 0.1 convolution_convert_fusion
  1.1 0.1 reshape.18
  1.2 0.1 reshape.19
  1.3 0.6 pad.4.mod_own
  1.9 116.5 %blocks.1 = bf16[2,256,1536]{2,1,0:T(8,128)(2,1)} custom-call(bf16[144,1536]{1,0:T(8,128)(2,1)} %bitcast.15, bf16[96,768]{1,0:T(8,128)(2,1)} %bitcast.16, bf16[16,128]{1,0:T(8,128)(2,1)} %pad.4.mod_own, bf16[2,256,1536]{2,1,0:T(8,128)(2,1)} %bitcast.14, s32[1,2]{1,0:T(1,128)} %shifts.1), custom_call_target="tpu_custom_call" | custom-call | tf_op jit(solution)/shard_map/blocks/pallas_call | solution.py:588
  118.4 2.7 %copy.11 = bf16[1,2,16,16,1536]{4,3,2,1,0:T(8,128)(2,1)} copy(bf16[1,2,16,16,1536]{4,3,2,1,0:T(8,128)(2,1)} %bitcast.13) | data formatting | bytes 3145728
  (3 shorter events, 0.1 us)
Async XLA Ops:
  0.0 0.9 copy-start

commit v6 on v5

--- a/solution.py
+++ b/solution.py
@@ -195,7 +195,7 @@
     rolled, normed, triples, att, rim, back, handed, result,
     sem_own, sem_send, sem_piece, sem_unit, sem_ms, sem_mr,
     sem_x, sem_hs, sem_hr, sem_bs, sem_br, sem_ps, sem_pr, sem_o, sem_fs, sem_fr, sem_gs,
-    sem_cs, sem_go,
+    sem_cs,
 ):
     row, col, y, core, x, z = place()
     section = lax.axis_index("section")
@@ -353,15 +353,6 @@
         for b in range(MB):
             own_state(b, result.at[b]).start()
 
-    def go():
-        pl.semaphore_signal(
-            sem_go, inc=1, device_id={"section": 1 - section}, device_id_type=MESH
-        )
-
-    @pl.when(section == 1)
-    def _():
-        pl.semaphore_wait(sem_go, 1)
-
     begin()
 
     mods[pl.ds(col, 1)] = mod_own[...][None]
@@ -400,7 +391,6 @@
 
         @pl.when(section == 0)
         def _():
-            go()
             for b in range(MB):
                 own_state(b, ext.at[b, pl.ds(0, 256), :]).wait()
                 pack_columns(b, ext[b, 0:256, :])
@@ -408,7 +398,6 @@
                     copy.start()
 
     plane(after_z)
-    rows()
     for k in range(1, 16):
         other = (col + k) % 16
         remote(mod_own, mods.at[other], sem_ms.at[k], sem_mr.at[other], peers[k - 1]).wait_recv()
@@ -514,6 +503,7 @@
         for b in range(MB):
             prepare(b)
 
+    rows()
     sides()
 
     @pl.when(section == 0)
@@ -544,12 +534,12 @@
     @pl.when(section == 1)
     def _():
         receive_first()
-        unpack(weights, 2304, out_rows)
         hand_gates().wait_recv()
         next_state(0)
         prepare(0)
         compute(0)
         next_state(1)
+        unpack(weights, 2304, out_rows)
         restore(0)
         project(0)
         prepare(1)
@@ -637,7 +627,6 @@
             dma((16,)),
             dma((2,)),
             dma((2 * MB,)),
-            pltpu.SemaphoreType.REGULAR,
         ],
         compiler_params=pltpu.CompilerParams(
             collective_id=0, has_side_effects=True, vmem_limit_bytes=60 << 20

time: 121 us -> 115 us (0.950)
  the two profiles are of different devices: /device:TPU:65 before, /device:TPU:89 now
where the time goes in v6:
time: 115 us
  Pallas kernels  110 us (96%)
  local copies, waits for them, and re-layouts  3.55 us (3%)
    pallas_call x1, Pallas kernels, blocks(): pl.pallas_call(block_kernel, out_shape=jax.ShapeDtypeStruct((MB, 256, D),...  110 us
    unnamed x3, local copies, waits for them, and re-layouts  2.76 us

profile of v6, /device:TPU:89, one launch (start us, length us, event | category | flops | bytes accessed | tf_op | source)
XLA Modules:
  0.0 114.8 jit_solution(2500683466938926123)
XLA Ops:
  0.0 0.0 copy-start
  0.0 0.7 convert_element_type.11
  0.7 0.1 multiply_cosine_fusion
  0.8 0.1 copy-done
  0.9 0.1 convolution_convert_fusion
  1.1 0.1 reshape.18
  1.2 0.1 reshape.19
  1.3 0.6 pad.4.mod_own
  1.9 110.3 %blocks.1 = bf16[2,256,1536]{2,1,0:T(8,128)(2,1)} custom-call(bf16[144,1536]{1,0:T(8,128)(2,1)} %bitcast.15, bf16[96,768]{1,0:T(8,128)(2,1)} %bitcast.16, bf16[16,128]{1,0:T(8,128)(2,1)} %pad.4.mod_own, bf16[2,256,1536]{2,1,0:T(8,128)(2,1)} %bitcast.14, s32[1,2]{1,0:T(1,128)} %shifts.1), custom_call_target="tpu_custom_call" | custom-call | tf_op jit(solution)/shard_map/blocks/pallas_call | solution.py:578
  112.2 2.7 %copy.11 = bf16[1,2,16,16,1536]{4,3,2,1,0:T(8,128)(2,1)} copy(bf16[1,2,16,16,1536]{4,3,2,1,0:T(8,128)(2,1)} %bitcast.13) | data formatting | bytes 3145728
  (3 shorter events, 0.1 us)
Async XLA Ops:
  0.0 0.9 copy-start
